TPU v7x, 32 devices: a whole 2x2x4 slice. The times are simulated.
32 devices in a mesh: grp: 2 (over x), dev: 16 (over z, y, core).
Axes of the slice: x: 2, y: 2, z: 4, core: 2. Of those that a mesh axis runs over, the one named last changes fastest.
Arguments:
- frames: float32 [2, 128, 512, 512], P('grp', 'dev'), may hold values from -6 to 6
- ref_spectrum: float32 [2, 128, 512, 512], P(None, None, 'dev'), as said below
- shifts: int32 [2, 3], replicated, may hold values from 0 to 127
- offsets: int32 [2, 3], replicated, may hold values from 0 to 127
Outputs:
- correlation: float32 [2, 128, 128, 128], P('grp', 'dev')
- new_reference: float32 [2, 128, 512, 512], P(None, 'grp', 'dev')
Inputs may be any that keep to these rules, and one draw needn't show every extreme that they name: `ref_spectrum`: real and imaginary parts are real numbers.
All inputs are finite; a program needn't handle non-finite values.
Results may differ from a plain program's by a relative error of at most 0.0001.
Values sent between devices are 32-bit elements; how exact they have to be, the bound alone decides.
No kernel may reach another device: no remote copies, remote signals or barrier semaphores. Data moves between devices by JAX's collectives and lax.ppermute only.
A program may use at most 192 MiB of HBM per device.

v0:
```python
import math

import jax
import jax.numpy as jnp
from jax import lax
from jax.sharding import PartitionSpec as P

NX = 512
NY = 512
NZ = 128
CROP = 128


def tables(length, outputs, offset):
    first = jnp.arange(outputs, dtype=jnp.int32) + offset
    second = jnp.arange(length, dtype=jnp.int32)
    phases = first[:, None] * second[None, :] % length
    angles = 2.0 * math.pi / length * phases.astype(jnp.float32)
    return (jnp.cos(angles), jnp.sin(angles))


def section(form, left_real, left_imag, cosine, sines, inverse):
    highest = lax.Precision.HIGHEST
    real_cos = jnp.einsum(form, left_real, cosine, precision=highest)
    imag_cos = jnp.einsum(form, left_imag, cosine, precision=highest)
    real_sin = jnp.einsum(form, left_real, sines, precision=highest)
    imag_sin = jnp.einsum(form, left_imag, sines, precision=highest)
    if inverse:
        return (real_cos - imag_sin, imag_cos + real_sin)
    return (real_cos + imag_sin, imag_cos - real_sin)


def real_section(form, left_real, left_imag, cosine, sines):
    highest = lax.Precision.HIGHEST
    return jnp.einsum(form, left_real, cosine, precision=highest) - jnp.einsum(
        form, left_imag, sines, precision=highest
    )


def local(frames, ref_spectrum, shifts, offsets):
    highest = lax.Precision.HIGHEST
    group = lax.axis_index("grp")
    device = lax.axis_index("dev")
    total = NZ * NY * NX
    factor = 1.0 / math.sqrt(total)
    frame = frames[0]
    drift = lax.dynamic_index_in_dim(shifts, group, 0, keepdims=False)
    corner = lax.dynamic_index_in_dim(offsets, group, 0, keepdims=False)
    cos_x, sin_x = tables(NX, NX, 0)
    plane_real = jnp.einsum("zyx,kx->zyk", frame, cos_x, precision=highest)
    plane_imag = -jnp.einsum("zyx,kx->zyk", frame, sin_x, precision=highest)
    cos_y, sin_y = tables(NY, NY, 0)
    plane_real, plane_imag = section("zyx,ky->zkx", plane_real, plane_imag, cos_y, sin_y, False)
    pencil_real, pencil_imag = (
        lax.all_to_all(plane_real, "dev", split_axis=1, concat_axis=0, tiled=True),
        lax.all_to_all(plane_imag, "dev", split_axis=1, concat_axis=0, tiled=True),
    )
    cos_z, sin_z = tables(NZ, NZ, 0)
    freq_real, freq_imag = section("zyx,kz->kyx", pencil_real, pencil_imag, cos_z, sin_z, False)
    freq_real = freq_real * factor
    freq_imag = freq_imag * factor
    rows_here = freq_real.shape[1]
    index_z = jnp.arange(NZ, dtype=jnp.int32)
    index_y = device * rows_here + jnp.arange(rows_here, dtype=jnp.int32)
    index_x = jnp.arange(NX, dtype=jnp.int32)
    turns_z = (index_z * drift[0] % NZ).astype(jnp.float32) / NZ
    turns_y = (index_y * drift[1] % NY).astype(jnp.float32) / NY
    turns_x = (index_x * drift[2] % NX).astype(jnp.float32) / NX
    angles = (
        2.0 * math.pi * (turns_z[:, None, None] + turns_y[None, :, None] + turns_x[None, None, :])
    )
    ramp_cos = jnp.cos(angles)
    ramp_sin = jnp.sin(angles)
    warped_real = freq_real * ramp_cos + freq_imag * ramp_sin
    warped_imag = freq_imag * ramp_cos - freq_real * ramp_sin
    summed_real, summed_imag = (
        lax.psum_scatter(0.25 * warped_real, "grp", scatter_dimension=0, tiled=True),
        lax.psum_scatter(0.25 * warped_imag, "grp", scatter_dimension=0, tiled=True),
    )
    half_rows = summed_real.shape[0]
    own_rows = lax.dynamic_slice_in_dim(ref_spectrum, group * half_rows, half_rows, axis=1)
    new_reference = jnp.stack([0.5 * own_rows[0] + summed_real, 0.5 * own_rows[1] + summed_imag])
    ref_real = ref_spectrum[0]
    ref_imag = ref_spectrum[1]
    cross_real = freq_real * ref_real + freq_imag * ref_imag
    cross_imag = freq_imag * ref_real - freq_real * ref_imag
    magnitude = jnp.sqrt(cross_real * cross_real + cross_imag * cross_imag)
    average = lax.psum(jnp.sum(magnitude), "dev") / total
    denominator = magnitude + average
    white_real = cross_real / denominator
    white_imag = cross_imag / denominator
    back_cos_z, back_sin_z = tables(NZ, CROP, corner[0])
    depth_real, depth_imag = section(
        "zyx,az->ayx", white_real, white_imag, back_cos_z, back_sin_z, True
    )
    back_cos_x, back_sin_x = tables(NX, CROP, corner[2])
    back_cos_y, back_sin_y = tables(NY, CROP, corner[1])
    width_real, width_imag = section(
        "zyx,ax->zya", depth_real, depth_imag, back_cos_x, back_sin_x, True
    )
    slab_real, slab_imag = (
        lax.all_to_all(width_real, "dev", split_axis=0, concat_axis=1, tiled=True),
        lax.all_to_all(width_imag, "dev", split_axis=0, concat_axis=1, tiled=True),
    )
    field = real_section("zyx,ay->zax", slab_real, slab_imag, back_cos_y, back_sin_y) * factor
    return (field[None], new_reference)


def solution(mesh):
    return jax.shard_map(
        local,
        mesh=mesh,
        in_specs=(P("grp", "dev", None, None), P(None, None, "dev", None), P(), P()),
        out_specs=(P("grp", "dev", None, None), P(None, "grp", "dev", None)),
        check_vma=False,
    )
```

profile of v0, /device:TPU:13, one launch (start us, length us, event | category | flops | bytes accessed | tf_op | source)
XLA Modules:
  0.0 822.1 jit_solution(11018444258257027897)
XLA Ops:
  7.2 28.5 %fusion.16 = f32[512,8,512]{2,0,1:T(8,128)S(1)} fusion(f32[1,8,512,512]{3,2,1,0:T(8,128)} %param.4), kind=kOutput, calls=%fused_computation.19 | convolution fusion | flops 12888571904 | bytes 16777216 | tf_op jit(solution)/shard_map/zyx,kx->zyk/dot_general | solution.py:51
  35.7 17.4 %fusion.18 = f32[512,8,512]{2,0,1:T(8,128)S(1)} fusion(f32[1,8,512,512]{3,2,1,0:T(8,128)S(1)} %copy-done.3), kind=kOutput, calls=%fused_computation.21 | convolution fusion | flops 12888571904 | bytes 16777216 | tf_op jit(solution)/shard_map/zyx,kx->zyk/dot_general | solution.py:50
  53.1 17.5 %fusion.10 = f32[512,8,512]{2,0,1:T(8,128)S(1)} fusion(f32[512,8,512]{2,0,1:T(8,128)S(1)} %fusion.16), kind=kOutput, calls=%fused_computation.13 | convolution fusion | flops 12890669056 | bytes 16777216 | tf_op jit(solution)/shard_map/zyx,ky->zkx/dot_general | solution.py:27
  70.7 17.8 %add_bitcast_fusion = f32[8,512,512]{2,1,0:T(8,128)S(1)} fusion(f32[512,8,512]{2,0,1:T(8,128)S(1)} %fusion.10, f32[512,8,512]{2,0,1:T(8,128)S(1)} %fusion.18), kind=kOutput, calls=%fused_computation.34 | convolution fusion | flops 12890669056 | bytes 25165824 | tf_op jit(solution)/shard_map/zyx,ky->zkx/dot_general | solution.py:24
  103.3 28.2 %fusion.8 = f32[512,8,512]{2,0,1:T(8,128)S(1)} fusion(f32[512,8,512]{2,0,1:T(8,128)} %copy-done.1), kind=kOutput, calls=%fused_computation.11 | convolution fusion | flops 12890669056 | bytes 16777216 | tf_op jit(solution)/shard_map/zyx,ky->zkx/dot_general | solution.py:25
  131.4 20.8 %subtract_bitcast_fusion = f32[8,512,512]{2,1,0:T(8,128)S(1)} fusion(f32[512,8,512]{2,0,1:T(8,128)S(1)} %fusion.8, f32[512,8,512]{2,0,1:T(8,128)} %copy-done), kind=kOutput, calls=%fused_computation.33 | convolution fusion | flops 12890669056 | bytes 25165824 | tf_op jit(solution)/shard_map/zyx,ky->zkx/dot_general | solution.py:26
  160.3 125.3 %all-to-all-done = f32[8,512,512]{2,0,1:T(8,128)} async-done(((f32[8,512,512]{2,0,1:T(8,128)}), f32[8,512,512]{2,0,1:T(8,128)}, u32[]{:S(2)}, u32[]{:S(2)}) %all-to-all-start) | async-done | bytes 8388640 | tf_op jit(solution)/shard_map/all_to_all | solution.py:55
  293.4 11.2 %fusion.233 = (f32[1,128,32,512]{3,2,1,0:T(8,128)}, f32[1,128,32,512]{3,2,1,0:T(8,128)}) fusion(f32[2,128,32,512]{3,2,1,0:T(8,128)} %param.5), kind=kLoop, calls=%fused_computation.251 | loop fusion | bytes 33554432 | tf_op jit(solution)/shard_map/slice | solution.py:83
  304.6 12.2 %fusion.2 = f32[128,32,512]{2,0,1:T(8,128)} fusion(f32[8,16,32,512]{3,0,2,1:T(8,128)} %bitcast.11), kind=kOutput, calls=%fused_computation.5 | convolution fusion | flops 3221454848 | bytes 16777216 | tf_op jit(solution)/shard_map/zyx,kz->kyx/dot_general | solution.py:24
  316.8 12.3 %fusion = f32[128,32,512]{2,0,1:T(8,128)} fusion(f32[8,16,32,512]{3,0,2,1:T(8,128)} %bitcast.11), kind=kOutput, calls=%fused_computation.3 | convolution fusion | flops 3221454848 | bytes 16777216 | tf_op jit(solution)/shard_map/zyx,kz->kyx/dot_general | solution.py:26
  329.1 143.7 %all-to-all-done.1 = f32[8,512,512]{2,0,1:T(8,128)} async-done(((f32[8,512,512]{2,0,1:T(8,128)}), f32[8,512,512]{2,0,1:T(8,128)}, u32[]{:S(2)}, u32[]{:S(2)}) %all-to-all-start.1) | async-done | bytes 8388640 | tf_op jit(solution)/shard_map/all_to_all | solution.py:56
  472.7 14.0 %add_multiply_fusion.2 = f32[128,32,512]{2,0,1:T(8,128)S(1)} fusion(f32[128,32,512]{2,0,1:T(8,128)} %fusion.2, f32[8,16,32,512]{3,0,2,1:T(8,128)} %bitcast.16), kind=kOutput, calls=%fused_computation.32 | convolution fusion | flops 3225649152 | bytes 25165824 | tf_op jit(solution)/shard_map/zyx,kz->kyx/dot_general | solution.py:27
  486.8 64.1 %add_multiply_fusion = (f32[128,32,512]{2,0,1:T(8,128)}, f32[128,32,512]{2,0,1:T(8,128)}, f32[]{:T(128)}, f32[128,32,512]{2,0,1:T(8,128)}, f32[128,32,512]{2,0,1:T(8,128)}) fusion(f32[128,32,512]{2,0,1:T(8,128)S(1)} %add_multiply_fusion.2, f32[512]{0:T(512)S(1)} %fusion.146, f32[128,32]{0,1:T(8,128)S(1)} %broadcast_add_fusion, ...), kind=kOutput, calls=%fused_computation.24 | convolution fusion | flops 3267362816 | bytes 75581440 | tf_op jit(solution)/shard_map/zyx,kz->kyx/dot_general | solution.py:25
  553.7 23.0 %psum.7 = f32[]{:T(128)} all-reduce(f32[]{:T(128)} %get-tuple-element.13), channel_id=1, replica_groups=mesh['grp'=2,'dev'=16] {'dev'}, use_global_device_ids=true, to_apply=%region_1.2 | all-reduce | flops 1 | bytes 8 | tf_op jit(solution)/shard_map/psum | solution.py:88
  577.2 16.7 %fusion.114 = f32[128,32,512]{2,0,1:T(8,128)S(1)} fusion(s32[128]{0:T(128)S(1)} %iota_add_fusion.1, f32[128,32,512]{2,0,1:T(8,128)} %get-tuple-element.15, f32[128,32,512]{2,0,1:T(8,128)} %get-tuple-element.14, f32[]{:T(128)S(6)} %div.27), kind=kOutput, calls=%fused_computation.123 | convolution fusion | flops 3231940608 | bytes 25166340 | tf_op jit(solution)/shard_map/zyx,az->ayx/dot_general | solution.py:26
  593.9 20.3 %fusion.122 = f32[128,32,512]{2,0,1:T(8,128)S(1)} fusion(s32[128]{0:T(128)S(1)} %iota_add_fusion.1, f32[128,32,512]{2,0,1:T(8,128)} %get-tuple-element.14, f32[128,32,512]{2,0,1:T(8,128)} %get-tuple-element.15, f32[]{:T(128)S(6)} %div.27), kind=kOutput, calls=%fused_computation.131 | convolution fusion | flops 3231940608 | bytes 25166340 | tf_op jit(solution)/shard_map/zyx,az->ayx/dot_general | solution.py:25
  622.0 15.5 %fusion.116 = f32[128,32,512]{2,0,1:T(8,128)S(1)} fusion(s32[128]{0:T(128)S(1)} %iota_add_fusion.1, f32[128,32,512]{2,0,1:T(8,128)S(1)} %bitcast.155, f32[128,32,512]{2,0,1:T(8,128)} %get-tuple-element.15, f32[]{:T(128)S(6)} %div.27), kind=kOutput, calls=%fused_computation.125 | convolution fusion | flops 3231940608 | bytes 25166340 | tf_op jit(solution)/shard_map/zyx,az->ayx/dot_general | solution.py:27
  637.5 18.5 %fusion.124 = f32[128,32,512]{2,0,1:T(8,128)S(1)} fusion(s32[128]{0:T(128)S(1)} %iota_add_fusion.1, f32[128,32,512]{2,0,1:T(8,128)} %get-tuple-element.15, f32[128,32,512]{2,0,1:T(8,128)S(1)} %bitcast.155, f32[]{:T(128)S(6)} %div.27), kind=kOutput, calls=%fused_computation.133 | convolution fusion | flops 3231940608 | bytes 25166340 | tf_op jit(solution)/shard_map/zyx,az->ayx/dot_general | solution.py:24
  666.5 15.0 %all-to-all-start.3 = ((f32[128,32,128]{2,1,0:T(8,128)}), f32[128,32,128]{2,1,0:T(8,128)S(1)}, u32[]{:S(2)}, u32[]{:S(2)}) async-start(f32[128,32,128]{2,1,0:T(8,128)} %copy.30), calls=%async_computation.3 | async-start | bytes 4194304 | tf_op jit(solution)/shard_map/all_to_all | solution.py:103
  681.5 12.8 %fusion.37 = f32[128,32,128]{2,0,1:T(8,128)S(1)} fusion(f32[128,32,512]{2,0,1:T(8,128)} %copy-done.8, f32[128,32,512]{2,0,1:T(8,128)} %copy-done.7, s32[128]{0:T(128)S(1)} %iota_add_fusion), kind=kOutput, calls=%fused_computation.54 | convolution fusion | flops 3224240128 | bytes 18874880 | tf_op jit(solution)/shard_map/zyx,ax->zya/dot_general | solution.py:27
  694.4 11.5 %fusion.51 = f32[128,32,128]{2,0,1:T(8,128)S(1)} fusion(f32[128,32,128]{2,0,1:T(8,128)S(1)} %fusion.37, f32[128,32,512]{2,0,1:T(8,128)S(1)} %copy-done.6, f32[128,32,512]{2,0,1:T(8,128)} %copy-done.4, s32[128]{0:T(128)S(1)} %iota_add_fusion), kind=kOutput, calls=%fused_computation.63 | convolution fusion | flops 3224764416 | bytes 20972032 | tf_op jit(solution)/shard_map/zyx,ax->zya/dot_general | solution.py:24
  708.4 20.8 %all-to-all-done.3 = f32[128,32,128]{2,1,0:T(8,128)S(1)} async-done(((f32[128,32,128]{2,1,0:T(8,128)}), f32[128,32,128]{2,1,0:T(8,128)S(1)}, u32[]{:S(2)}, u32[]{:S(2)}) %all-to-all-start.3) | async-done | bytes 2097184 | tf_op jit(solution)/shard_map/all_to_all | solution.py:103
  734.7 8.6 %constant_dynamic-slice_fusion = (f32[1,64,32,512]{3,2,1,0:T(8,128)}, f32[1,64,32,512]{3,2,1,0:T(8,128)}) fusion(f32[2,128,32,512]{3,2,1,0:T(8,128)} %param.5, s32[]{:T(128)S(6)} %select_n.89, s32[]{:T(128)S(6)} %add.231), kind=kLoop, calls=%fused_computation.175 | loop fusion | bytes 16777224 | tf_op jit(solution)/shard_map/slice | solution.py:82
  744.8 36.3 %all-to-all-done.2 = f32[128,32,128]{2,1,0:T(8,128)} async-done(((f32[128,32,128]{2,1,0:T(8,128)}), f32[128,32,128]{2,1,0:T(8,128)}, u32[]{:S(2)}, u32[]{:S(2)}) %all-to-all-start.2) | async-done | bytes 2097184 | tf_op jit(solution)/shard_map/all_to_all | solution.py:102
  (63 shorter events, 94.9 us)
Async XLA Ops:
  7.2 28.5 %copy-start.3 = (f32[1,8,512,512]{3,2,1,0:T(8,128)S(1)}, f32[1,8,512,512]{3,2,1,0:T(8,128)}, u32[]{:S(2)}) copy-start(f32[1,8,512,512]{3,2,1,0:T(8,128)} %param.4) | copy-start | bytes 25165828
  35.7 17.4 %copy-start.1 = (f32[512,8,512]{2,0,1:T(8,128)}, f32[512,8,512]{2,0,1:T(8,128)S(1)}, u32[]{:S(2)}) copy-start(f32[512,8,512]{2,0,1:T(8,128)S(1)} %fusion.16) | copy-start | bytes 25165828
  53.1 17.6 %copy-start = (f32[512,8,512]{2,0,1:T(8,128)}, f32[512,8,512]{2,0,1:T(8,128)S(1)}, u32[]{:S(2)}) copy-start(f32[512,8,512]{2,0,1:T(8,128)S(1)} %fusion.18) | copy-start | bytes 25165828
  96.7 188.9 %all-to-all-start = ((f32[8,512,512]{2,0,1:T(8,128)}), f32[8,512,512]{2,0,1:T(8,128)}, u32[]{:S(2)}, u32[]{:S(2)}) async-start(f32[8,512,512]{2,0,1:T(8,128)} %copy.20), calls=%async_computation | async-start | bytes 16777216 | tf_op jit(solution)/shard_map/all_to_all | solution.py:55
  160.3 130.1 %copy-start.10 = (s32[2,3]{1,0:T(2,128)S(1)}, s32[2,3]{1,0:T(2,128)}, u32[]{:S(2)}) copy-start(s32[2,3]{1,0:T(2,128)} %param.6) | copy-start | bytes 76
  160.3 130.1 %copy-start.11 = (s32[2,3]{1,0:T(2,128)S(1)}, s32[2,3]{1,0:T(2,128)}, u32[]{:S(2)}) copy-start(s32[2,3]{1,0:T(2,128)} %param.7) | copy-start | bytes 76
  285.6 187.1 %all-to-all-start.1 = ((f32[8,512,512]{2,0,1:T(8,128)}), f32[8,512,512]{2,0,1:T(8,128)}, u32[]{:S(2)}, u32[]{:S(2)}) async-start(f32[8,512,512]{2,0,1:T(8,128)} %copy.24), calls=%async_computation.1 | async-start | bytes 16777216 | tf_op jit(solution)/shard_map/all_to_all | solution.py:56
  290.4 499.5 %reduce-scatter.5.cloned.1.call-start = ((), (), s32[]{:S(2)}) async-start(), calls=%async_computation.7 | async-start | bytes 12582912 | tf_op jit(solution)/shard_map/reduce_scatter | solution.py:78
  472.7 14.0 %copy-start.2 = (f32[128,32,512]{2,0,1:T(8,128)S(1)}, f32[128,32,512]{2,0,1:T(8,128)}, u32[]{:S(2)}) copy-start(f32[128,32,512]{2,0,1:T(8,128)} %fusion) | copy-start | bytes 25165828
  550.9 247.4 %reduce-scatter.3.cloned.1.call-start = ((), (), s32[]{:S(2)}) async-start(), calls=%async_computation.6 | async-start | bytes 12582912 | tf_op jit(solution)/shard_map/reduce_scatter | solution.py:77
  577.2 44.7 %slice-start = ((s8[8388608]{0:T(1024)(128)(4,1)}), s8[4194304]{0:T(1024)(128)(4,1)S(1)}, s32[]{:S(2)}) async-start(s8[8388608]{0:T(1024)(128)(4,1)} %bitcast.154), calls=%async_computation.8 | async-start | bytes 8388608
  593.9 20.4 %copy-start.7 = (f32[128,32,512]{2,0,1:T(8,128)}, f32[128,32,512]{2,0,1:T(8,128)S(1)}, u32[]{:S(2)}) copy-start(f32[128,32,512]{2,0,1:T(8,128)S(1)} %fusion.114) | copy-start | bytes 25165828
  593.9 28.1 %slice-start.1 = ((s8[8388608]{0:T(1024)(128)(4,1)}), s8[4194304]{0:T(1024)(128)(4,1)S(1)}, s32[]{:S(2)}) async-start(s8[8388608]{0:T(1024)(128)(4,1)} %bitcast.154), calls=%async_computation.9 | async-start | bytes 8388608
  614.3 7.7 copy-start.8
  637.5 18.6 %copy-start.4 = (f32[128,32,512]{2,0,1:T(8,128)}, f32[128,32,512]{2,0,1:T(8,128)S(1)}, u32[]{:S(2)}) copy-start(f32[128,32,512]{2,0,1:T(8,128)S(1)} %fusion.116) | copy-start | bytes 25165828
  656.1 7.9 copy-start.5
  666.5 62.7 %all-to-all-start.3 = ((f32[128,32,128]{2,1,0:T(8,128)}), f32[128,32,128]{2,1,0:T(8,128)S(1)}, u32[]{:S(2)}, u32[]{:S(2)}) async-start(f32[128,32,128]{2,1,0:T(8,128)} %copy.30), calls=%async_computation.3 | async-start | bytes 4194304 | tf_op jit(solution)/shard_map/all_to_all | solution.py:103
  681.5 12.9 %copy-start.6 = (f32[128,32,512]{2,0,1:T(8,128)S(1)}, f32[128,32,512]{2,0,1:T(8,128)}, u32[]{:S(2)}) copy-start(f32[128,32,512]{2,0,1:T(8,128)} %copy-done.5) | copy-start | bytes 25165828
  729.2 51.9 %all-to-all-start.2 = ((f32[128,32,128]{2,1,0:T(8,128)}), f32[128,32,128]{2,1,0:T(8,128)}, u32[]{:S(2)}, u32[]{:S(2)}) async-start(f32[128,32,128]{2,1,0:T(8,128)} %copy.28), calls=%async_computation.2 | async-start | bytes 4194304 | tf_op jit(solution)/shard_map/all_to_all | solution.py:102
  798.3 6.7 copy-start.9
Sparse Core Ops, SparseCore 0:
  551.0 98.5 reduce-scatter.4
  652.5 99.3 reduce-scatter.2
where the time goes:
time: 831 us; the launch traced here: 822 us
  matrix products  351 us (42%)
  waiting for transfers between devices  327 us (39%)
  local copies, waits for them, and re-layouts  54.2 us (7%)
  starting transfers between devices  31.1 us (4%)
  blocking collectives  23 us (3%)
  other arithmetic  21.1 us (3%)
  between operations  15.3 us (2%)
    all_to_all x1, waiting for transfers between devices, local(): lax.all_to_all(plane_imag, 'dev', split_axis=1, concat_axis=0, tiled=True)  144 us
    all_to_all x1, waiting for transfers between devices, local(): lax.all_to_all(plane_real, 'dev', split_axis=1, concat_axis=0, tiled=True)  125 us
    dot_general x4, matrix products, section(): imag_cos = jnp.einsum(form, left_imag, cosine, precision=highest)  120 us
    dot_general x4, matrix products, section(): real_cos = jnp.einsum(form, left_real, cosine, precision=highest)  60 us
    dot_general x4, matrix products, section(): imag_sin = jnp.einsum(form, left_imag, sines, precision=highest)  59.9 us
    dot_general x4, matrix products, section(): real_sin = jnp.einsum(form, left_real, sines, precision=highest)  57.6 us
    all_to_all x1, waiting for transfers between devices, local(): lax.all_to_all(width_real, 'dev', split_axis=0, concat_axis=1, tiled=True)  36.3 us
    dot_general x1, matrix products, local(): plane_imag = -jnp.einsum('zyx,kx->zyk', frame, sin_x, precision=highest)  28.5 us
  transfers between devices with their start and end apart: 6, of which 4 were waited for; matrix products, arithmetic and copies ran while one was open for 29% of the time, Pallas kernels for 0%

commit v1 on v0

v1 whole, which is shorter than its diff:
```python
import functools
import math

import jax
import jax.numpy as jnp
import ml_dtypes
import numpy as np
from jax import lax
from jax.experimental import pallas as pl
from jax.experimental.pallas import tpu as pltpu
from jax.sharding import PartitionSpec as P

CROP = 128
LANES = 128
ROWS = 8
F32 = jnp.float32
BF16 = jnp.bfloat16


def fixed_wave(length):
    phases = np.outer(np.arange(length), np.arange(length)) % length
    angles = 2.0 * np.pi / length * phases
    table = np.concatenate([np.cos(angles), np.sin(angles)], 0).astype(np.float32)
    high = table.astype(ml_dtypes.bfloat16)
    low = (table - high.astype(np.float32)).astype(ml_dtypes.bfloat16)
    return np.stack([high, low])


def wave(rows, columns, length):
    phases = rows[:, None] * columns[None, :] % length
    angles = 2.0 * math.pi / length * phases.astype(F32)
    return (jnp.cos(angles), jnp.sin(angles))


def ramp(index, drift, length):
    angles = 2.0 * math.pi / length * (index * drift % length).astype(F32)
    return (jnp.cos(angles), jnp.sin(angles))


def halves(table):
    high = lax.reduce_precision(table, 8, 7)
    return jnp.stack([high.astype(BF16), (table - high).astype(BF16)])


def parts(value):
    high = value.astype(BF16)
    return high, (value - high.astype(F32)).astype(BF16)


def dot3(left, right):
    return jnp.dot(
        jnp.concatenate([left[0], left[0], left[1]], 1),
        jnp.concatenate([right[0], right[1], right[0]], 0),
        preferred_element_type=F32,
    )


def forward_kernel(frame, table_x, table_y, *refs):
    out = refs[-1]
    count, ny, nx = frame.shape
    devices, _, _, rows, _ = out.shape
    column = [jnp.concatenate([table_x[i, :nx, :], table_x[i, nx:, :]], 1) for i in range(2)]
    for z in range(count):
        plane = parts(dot3(parts(frame[z]), column))
        both = dot3((table_y[0], table_y[1]), plane)
        real = both[:ny, :LANES] - both[ny:, LANES:]
        imag = -both[:ny, LANES:] - both[ny:, :LANES]
        out[:, 0, z] = real.reshape(devices, rows, LANES)
        out[:, 1, z] = imag.reshape(devices, rows, LANES)


def middle_kernel(group, got, table, ref_own, ref_far, turn_z, turn_yx, cross, size, own, far, sums):
    del group
    nz = cross.shape[2]
    half = own.shape[1]
    flat = got.reshape(2 * nz * ROWS, LANES)
    near = ref_own.reshape(2 * half * ROWS, LANES)
    away = ref_far.reshape(2 * half * ROWS, LANES)
    own_flat = own.reshape(2 * half * ROWS, LANES)
    far_flat = far.reshape(2 * half * ROWS, LANES)
    matrix = (table[0], table[1])
    zc, zs = turn_z[0], turn_z[1]
    total = jnp.zeros((8, LANES), F32)
    for pair in range(0, ROWS, 2):
        taken = [flat[pl.ds(r, 2 * nz, stride=ROWS), :] for r in (pair, pair + 1)]
        freq = dot3(matrix, parts(jnp.concatenate(taken, 1)))
        for r in (pair, pair + 1):
            at = slice((r - pair) * LANES, (r - pair + 1) * LANES)
            fr, fi = freq[:nz, at], freq[nz:, at]
            yc, ys = turn_yx[0, r : r + 1, :], turn_yx[1, r : r + 1, :]
            ar, ai = fr * zc + fi * zs, fi * zc - fr * zs
            wr, wi = ar * yc + ai * ys, ai * yc - ar * ys
            own_part = [near[pl.ds(p * half * ROWS + r, half, stride=ROWS), :] for p in range(2)]
            far_part = [away[pl.ds(p * half * ROWS + r, half, stride=ROWS), :] for p in range(2)]
            for p, w in enumerate((wr, wi)):
                where = pl.ds(p * half * ROWS + r, half, stride=ROWS)
                own_flat[where, :] = w[:half] + 0.5 * own_part[p]
                far_flat[where, :] = w[half:]
            rr = jnp.concatenate([own_part[0], far_part[0]], 0)
            ri = jnp.concatenate([own_part[1], far_part[1]], 0)
            cr = fr * rr + fi * ri
            ci = fi * rr - fr * ri
            cross[r, 0] = cr
            cross[r, 1] = ci
            magnitude = jnp.sqrt(cr * cr + ci * ci)
            size[r] = magnitude
            total = total + jnp.sum(magnitude.reshape(nz // 8, 8, LANES), 0)
    sums[0] = total


def inverse_kernel(average, *refs):
    table_x, table_z, out = refs[-3:]
    crosses, sizes = refs[: len(refs) // 2 - 1], refs[len(refs) // 2 - 1 : -3]
    nz = crosses[0].shape[2]
    mean = average[0]
    flat = out.reshape(2 * CROP * ROWS, LANES)
    matrix = (table_z[0], table_z[1])
    width = None
    for c, (cross, size) in enumerate(zip(crosses, sizes)):
        scale = 1.0 / (size[...] + mean)
        white = jnp.concatenate(
            [(cross[:, p] * scale).reshape(ROWS * nz, LANES) for p in range(2)], 1
        )
        at = slice(c * 2 * LANES, (c + 1) * 2 * LANES)
        piece = dot3(parts(white), (table_x[0, at, :], table_x[1, at, :]))
        width = piece if width is None else width + piece
    for pair in range(0, ROWS, 2):
        stacked = jnp.concatenate(
            [
                jnp.concatenate([width[r * nz : (r + 1) * nz, :CROP], width[r * nz : (r + 1) * nz, CROP:]], 0)
                for r in (pair, pair + 1)
            ],
            1,
        )
        depth = dot3(matrix, parts(stacked))
        flat[pl.ds(pair, 2 * CROP, stride=ROWS), :] = depth[:, :CROP]
        flat[pl.ds(pair + 1, 2 * CROP, stride=ROWS), :] = depth[:, CROP:]


def total_over(value, axis, size):
    if size & (size - 1):
        return lax.psum(value, axis)
    step = 1
    while step < size:
        flips = (1, 2, 3) if 2 * step < size else (1,)
        pairs = [[(i, i ^ (flip * step)) for i in range(size)] for flip in flips]
        value = value + sum(lax.ppermute(value, axis, pair) for pair in pairs)
        step *= len(flips) + 1
    return value


def local(frames, ref_spectrum, shifts, offsets, *, groups, devices):
    group = lax.axis_index("grp")
    device = lax.axis_index("dev")
    _, planes, ny, nx = frames.shape
    _, nz, rows, _ = ref_spectrum.shape
    total = nz * ny * nx
    factor = 1.0 / math.sqrt(total)
    half = nz // groups
    chunks = nx // LANES
    frame = frames[0]
    ints = lambda count: jnp.arange(count, dtype=jnp.int32)
    whole = lambda shape: pl.BlockSpec(shape, lambda *_: (0,) * len(shape))

    table_x = jnp.asarray(fixed_wave(nx))
    table_y = table_x if ny == nx else jnp.asarray(fixed_wave(ny))

    def send(c, *after):
        return pl.pallas_call(
            forward_kernel,
            grid=(planes // 2,),
            in_specs=[
                pl.BlockSpec((2, ny, nx), lambda z: (z, 0, 0)),
                pl.BlockSpec((2, 2 * nx, LANES), lambda z: (0, 0, c)),
                whole((2, 2 * ny, ny)),
            ]
            + [pl.BlockSpec(memory_space=pl.ANY)] * len(after),
            out_specs=pl.BlockSpec((devices, 2, 2, rows, LANES), lambda z: (0, 0, z, 0, 0)),
            out_shape=jax.ShapeDtypeStruct((devices, 2, planes, rows, LANES), F32),
            name=f"forward_{c}",
        )(frame, table_x, table_y, *after)

    def exchange(packed):
        return lax.all_to_all(packed, "dev", split_axis=0, concat_axis=0, tiled=True)

    first = send(0)
    shifts, offsets, first = lax.optimization_barrier((shifts, offsets, first))
    drift = lax.dynamic_index_in_dim(shifts, group, 0, keepdims=False)
    corner = lax.dynamic_index_in_dim(offsets, group, 0, keepdims=False)
    kz = (ints(nz) + group * half) % nz
    ky = device * rows + ints(rows)
    cos_z, sin_z = wave(kz, ints(nz), nz)
    split = lambda table: table.reshape(nz, devices, planes)
    table_z = halves(
        factor
        * jnp.stack(
            [
                jnp.stack([split(cos_z), split(sin_z)], 2),
                jnp.stack([-split(sin_z), split(cos_z)], 2),
            ]
        ).reshape(2 * nz, 2 * nz)
    )
    cz, sz = ramp(kz, drift[0], nz)
    turn_z = jnp.broadcast_to(jnp.stack([cz, sz])[:, :, None], (2, nz, LANES))
    cy, sy = ramp(ky, drift[1], ny)
    cx, sx = ramp(ints(nx), drift[2], nx)
    turn_yx = 0.25 * jnp.stack(
        [cy[:, None] * cx - sy[:, None] * sx, sy[:, None] * cx + cy[:, None] * sx]
    )
    ref_view = ref_spectrum.reshape(2, groups, half, rows, nx)
    group_number = group.astype(jnp.int32).reshape(1)
    steps = rows // ROWS

    def middle(got, c):
        return pl.pallas_call(
            middle_kernel,
            grid_spec=pltpu.PrefetchScalarGridSpec(
                num_scalar_prefetch=1,
                grid=(steps,),
                in_specs=[
                    pl.BlockSpec((2 * nz, ROWS, LANES), lambda i, g: (0, i, 0)),
                    whole((2, 2 * nz, 2 * nz)),
                    pl.BlockSpec((2, 1, half, ROWS, LANES), lambda i, g: (0, g[0], 0, i, c)),
                    pl.BlockSpec((2, 1, half, ROWS, LANES), lambda i, g: (0, groups - 1 - g[0], 0, i, c)),
                    whole((2, nz, LANES)),
                    pl.BlockSpec((2, ROWS, LANES), lambda i, g: (0, i, c)),
                ],
                out_specs=[
                    pl.BlockSpec((ROWS, 2, nz, LANES), lambda i, g: (i, 0, 0, 0)),
                    pl.BlockSpec((ROWS, nz, LANES), lambda i, g: (i, 0, 0)),
                    pl.BlockSpec((2, half, ROWS, LANES), lambda i, g: (0, 0, i, 0)),
                    pl.BlockSpec((2, half, ROWS, LANES), lambda i, g: (0, 0, i, 0)),
                    pl.BlockSpec((1, 8, LANES), lambda i, g: (i, 0, 0)),
                ],
            ),
            out_shape=[
                jax.ShapeDtypeStruct((rows, 2, nz, LANES), F32),
                jax.ShapeDtypeStruct((rows, nz, LANES), F32),
                jax.ShapeDtypeStruct((2, half, rows, LANES), F32),
                jax.ShapeDtypeStruct((2, half, rows, LANES), F32),
                jax.ShapeDtypeStruct((steps, 8, LANES), F32),
            ],
            name=f"middle_{c}",
        )(group_number, got, table_z, ref_view, ref_view, turn_z, turn_yx)

    crosses, sizes, owns, fars, sums = [], [], [], [], []
    swap = [(i, groups - 1 - i) for i in range(groups)]
    packed = [first]
    for c in range(chunks):
        if c + 1 < chunks:
            packed.append(send(c + 1, packed[c], *sums[-1:]))
        if c > 1:
            packed[c], fars[c - 2] = lax.optimization_barrier((packed[c], fars[c - 2]))
        got = exchange(packed[c]).reshape(2 * nz, rows, LANES)
        if c > 0 and c == chunks - 1:
            got, fars[c - 1] = lax.optimization_barrier((got, fars[c - 1]))
        cross, size, own, far, part = middle(got, c)
        sizes.append(size)
        crosses.append(cross)
        owns.append(own)
        fars.append(lax.ppermute(far, "grp", swap))
        sums.append(part)
    mass = jnp.sum(sum(sums))
    average = total_over(mass, "dev", devices) / total

    take_x = (ints(CROP) + corner[2]) % nx
    take_y = (ints(CROP) + corner[1]) % ny
    take_z = (ints(CROP) + corner[0]) % nz
    cb, sb = wave(ints(nx), take_x, nx)
    lanes = lambda table: table.reshape(chunks, LANES, CROP)
    cb, sb = lanes(cb), lanes(sb)
    back_x = halves(
        jnp.stack(
            [jnp.concatenate([cb, sb], 2), jnp.concatenate([-sb, cb], 2)], 1
        ).reshape(2 * nx, 2 * CROP)
    )
    bz, dz = wave(take_z, kz, nz)
    back_z = halves(
        jnp.stack(
            [jnp.concatenate([bz, -dz], 1), jnp.concatenate([dz, bz], 1)], 1
        ).reshape(2 * CROP, 2 * nz)
    )
    cos_b, sin_b = wave(take_y, ints(ny), ny)
    back_y = factor * jnp.stack(
        [cos_b.reshape(CROP, devices, rows), -sin_b.reshape(CROP, devices, rows)], 2
    )
    back = pl.pallas_call(
        inverse_kernel,
        grid=(steps,),
        in_specs=[pl.BlockSpec(memory_space=pltpu.SMEM)]
        + [pl.BlockSpec((ROWS, 2, nz, LANES), lambda i: (i, 0, 0, 0))] * chunks
        + [pl.BlockSpec((ROWS, nz, LANES), lambda i: (i, 0, 0))] * chunks
        + [whole((2, 2 * nx, 2 * CROP)), whole((2, 2 * CROP, 2 * nz))],
        out_specs=pl.BlockSpec((2 * CROP, ROWS, LANES), lambda i: (0, i, 0)),
        out_shape=jax.ShapeDtypeStruct((2 * CROP, rows, LANES), F32),
        name="inverse",
    )(average.reshape(1), *crosses, *sizes, back_x, back_z)
    slab = exchange(back.reshape(devices, CROP // devices, 2, rows, CROP))
    field = jnp.einsum("szprx,yspr->zyx", slab, back_y, precision=lax.Precision.HIGH)
    new_reference = jnp.concatenate([own + far for own, far in zip(owns, fars)], 3)
    return (field[None], new_reference)


def solution(mesh):
    body = functools.partial(local, groups=mesh.shape["grp"], devices=mesh.shape["dev"])
    return jax.shard_map(
        body,
        mesh=mesh,
        in_specs=(P("grp", "dev", None, None), P(None, None, "dev", None), P(), P()),
        out_specs=(P("grp", "dev", None, None), P(None, "grp", "dev", None)),
        check_vma=False,
    )
```

time: 831 us -> 559 us (0.67)
  matrix products: 351 us -> 4.29 us
  Pallas kernels: 0 us -> 127 us
  local copies, waits for them, and re-layouts: 54.2 us -> 4.56 us
  waiting for transfers between devices: 327 us -> 353 us
  blocking collectives: 23 us -> 0 us
  starting transfers between devices: 31.1 us -> 43.6 us
  between operations: 15.3 us -> 5.28 us
    dot_general x20 -> x1, matrix products: 351 us -> 4.29 us  [local(): jnp.einsum('szprx,yspr->zyx', slab, back_y, precision=lax.Precision.HIGH)]
    pallas_call x0 -> x9, Pallas kernels: none -> 127 us  [the longest x4 69.3 us: send(): pl.pallas_call(forward_kernel, grid=(planes // 2,), in_specs=[pl.BlockSpe...]
    ppermute x0 -> x10, waiting for transfers between devices: none -> 98.5 us  [the longest x4 97 us: local(): fars.append(lax.ppermute(far, 'grp', swap))]
    all_to_all x4 -> x5, waiting for transfers between devices: 326 us -> 255 us  [exchange(): lax.all_to_all(packed, 'dev', split_axis=0, concat_axis=0, tiled=True)]
    psum x1 -> x0, blocking collectives: 23 us -> none  [local(): average = lax.psum(jnp.sum(magnitude), 'dev') / total]
    slice x4 -> x2, local copies, waits for them, and re-layouts: 21.2 us -> 1.29 us  [the longest x1 0.65 us: local(): take_y = (ints(CROP) + corner[1]) % ny]
    another operation x3 -> x9, other arithmetic: 16.9 us -> 3.01 us  [the longest x3 2.55 us: halves(): return jnp.stack([high.astype(BF16), (table - high).astype(BF16)])]
    ppermute x0 -> x10, starting transfers between devices: none -> 12.1 us  [the longest x6 7.02 us: total_over(): value = value + sum((lax.ppermute(value, axis, pair) for pair in pairs))]
  transfers between devices with their start and end apart: 6 -> 15, of which waited for: 4 -> 11; matrix products, arithmetic and copies ran while one was open for 29% -> 4% of each run, Pallas kernels for 0% -> 15%
where the time goes in v1:
time: 559 us; the launch traced here: 558 us
  waiting for transfers between devices  353 us (63%)
  Pallas kernels  127 us (23%)
  starting transfers between devices  43.6 us (8%)
  other arithmetic  20 us (4%)
    all_to_all x5, waiting for transfers between devices, exchange(): lax.all_to_all(packed, 'dev', split_axis=0, concat_axis=0, tiled=True)  255 us
    ppermute x4, waiting for transfers between devices, local(): fars.append(lax.ppermute(far, 'grp', swap))  97 us
    pallas_call x4, Pallas kernels, send(): pl.pallas_call(forward_kernel, grid=(planes // 2,), in_specs=[pl.BlockSpe...  69.3 us
    pallas_call x4, Pallas kernels, middle(): pl.pallas_call(middle_kernel, grid_spec=pltpu.PrefetchScalarGridSpec(num_...  41 us
    all_to_all x5, starting transfers between devices, exchange(): lax.all_to_all(packed, 'dev', split_axis=0, concat_axis=0, tiled=True)  31.5 us
    pallas_call x1, Pallas kernels, local(): pl.pallas_call(inverse_kernel, grid=(steps,), in_specs=[pl.BlockSpec(memo...  17 us
  transfers between devices with their start and end apart: 15, of which 11 were waited for; matrix products, arithmetic and copies ran while one was open for 4% of the time, Pallas kernels for 15%

profile of v1, /device:TPU:13, one launch (start us, length us, event | category | flops | bytes accessed | tf_op | source)
XLA Modules:
  0.0 558.0 jit_solution(10380101142633510119)
XLA Ops:
  0.6 17.3 %forward_0.1.refs_0_ = f32[16,2,8,32,128]{4,3,2,1,0:T(8,128)} custom-call(f32[8,512,512]{2,1,0:T(8,128)} %bitcast.51, bf16[2,1024,512]{2,1,0:T(8,128)(2,1)} %constant.146.clone.table_x.table_y, bf16[2,1024,512]{2,1,0:T(8,128)(2,1)} %constant.146.clone.table_x.table_y), custom_call_target="tpu_custom_call" | custom-call | tf_op jit(solution)/shard_map/forward_0/pallas_call | solution.py:169
  17.9 6.5 %all-to-all-start = ((f32[16,2,8,32,128]{4,3,2,1,0:T(8,128)}), f32[16,2,8,32,128]{4,3,2,1,0:T(8,128)}, u32[]{:S(2)}, u32[]{:S(2)}) async-start(f32[16,2,8,32,128]{4,3,2,1,0:T(8,128)} %forward_0.1.refs_0_), calls=%async_computation | async-start | bytes 8388608 | tf_op jit(solution)/shard_map/all_to_all | solution.py:184
  24.4 17.4 %forward_1.1.refs_0_ = f32[16,2,8,32,128]{4,3,2,1,0:T(8,128)} custom-call(f32[8,512,512]{2,1,0:T(8,128)} %bitcast.52, bf16[2,1024,512]{2,1,0:T(8,128)(2,1)} %constant.146.clone.table_x.table_y, bf16[2,1024,512]{2,1,0:T(8,128)(2,1)} %constant.146.clone.table_x.table_y, f32[16,2,8,32,128]{4,3,2,1,0:T(8,128)} %forward_0.1.refs_0_), custom_call_target="tpu_custom_call" | custom-call | tf_op jit(solution)/shard_map/forward_1/pallas_call | solution.py:169
  41.8 75.1 %all-to-all-done = f32[16,2,8,32,128]{4,3,2,1,0:T(8,128)} async-done(((f32[16,2,8,32,128]{4,3,2,1,0:T(8,128)}), f32[16,2,8,32,128]{4,3,2,1,0:T(8,128)}, u32[]{:S(2)}, u32[]{:S(2)}) %all-to-all-start) | async-done | bytes 4194336 | tf_op jit(solution)/shard_map/all_to_all | solution.py:184
  116.9 4.8 all-to-all-start.1
  129.1 10.0 %middle_0.1 = (f32[32,2,128,128]{3,2,1,0:T(8,128)}, f32[32,128,128]{2,1,0:T(8,128)}, f32[2,64,32,128]{3,2,1,0:T(8,128)}, f32[2,64,32,128]{3,2,1,0:T(8,128)}, f32[4,8,128]{2,1,0:T(8,128)}) custom-call(s32[1]{0:T(128)} %bitcast.4.group, f32[256,32,128]{2,1,0:T(8,128)} %bitcast.5.got, bf16[2,256,256]{2,1,0:T(8,128)(2,1)} %pad_maximum_fusion.3.table, ...), custom_call_target="tpu_custom_call" | custom-call | tf_op jit(solution)/shard_map/middle_0/pallas_call | solution.py:215
  140.4 17.3 %forward_2.1.refs_0_ = f32[16,2,8,32,128]{4,3,2,1,0:T(8,128)} custom-call(f32[8,512,512]{2,1,0:T(8,128)} %bitcast.53, bf16[2,1024,512]{2,1,0:T(8,128)(2,1)} %constant.146.clone.table_x.table_y, bf16[2,1024,512]{2,1,0:T(8,128)(2,1)} %constant.146.clone.table_x.table_y, f32[16,2,8,32,128]{4,3,2,1,0:T(8,128)} %forward_1.1.refs_0_, ...), custom_call_target="tpu_custom_call" | custom-call | tf_op jit(solution)/shard_map/forward_2/pallas_call | solution.py:169
  157.7 28.6 %collective-permute-done = f32[2,64,32,128]{3,2,1,0:T(8,128)S(1)} collective-permute-done((f32[2,64,32,128]{3,2,1,0:T(8,128)}, f32[2,64,32,128]{3,2,1,0:T(8,128)S(1)}, u32[]{:S(2)}, u32[]{:S(2)}) %collective-permute-start) | collective-permute-done | bytes 2097184 | tf_op jit(solution)/shard_map/ppermute | solution.py:261
  186.3 27.9 %all-to-all-done.1 = f32[16,2,8,32,128]{4,3,2,1,0:T(8,128)} async-done(((f32[16,2,8,32,128]{4,3,2,1,0:T(8,128)}), f32[16,2,8,32,128]{4,3,2,1,0:T(8,128)}, u32[]{:S(2)}, u32[]{:S(2)}) %all-to-all-start.1) | async-done | bytes 4194336 | tf_op jit(solution)/shard_map/all_to_all | solution.py:184
  214.2 4.8 all-to-all-start.2
  218.9 10.1 %middle_1.1 = (f32[32,2,128,128]{3,2,1,0:T(8,128)}, f32[32,128,128]{2,1,0:T(8,128)}, f32[2,64,32,128]{3,2,1,0:T(8,128)}, f32[2,64,32,128]{3,2,1,0:T(8,128)}, f32[4,8,128]{2,1,0:T(8,128)}) custom-call(s32[1]{0:T(128)} %bitcast.4.group, f32[256,32,128]{2,1,0:T(8,128)} %bitcast.13.got, bf16[2,256,256]{2,1,0:T(8,128)(2,1)} %pad_maximum_fusion.3.table, ...), custom_call_target="tpu_custom_call" | custom-call | tf_op jit(solution)/shard_map/middle_1/pallas_call | solution.py:215
  230.3 17.4 %forward_3.1 = f32[16,2,8,32,128]{4,3,2,1,0:T(8,128)} custom-call(f32[8,512,512]{2,1,0:T(8,128)} %bitcast.54, bf16[2,1024,512]{2,1,0:T(8,128)(2,1)} %constant.146.clone.table_x.table_y, bf16[2,1024,512]{2,1,0:T(8,128)(2,1)} %constant.146.clone.table_x.table_y, f32[16,2,8,32,128]{4,3,2,1,0:T(8,128)} %forward_2.1.refs_0_, f32[4,8,128]{2,1,0:T(8,128)} %get-tuple-element.35.refs_1_), custom_call_target="tpu_custom_call" | custom-call | tf_op jit(solution)/shard_map/forward_3/pallas_call | solution.py:169
  247.7 28.5 %collective-permute-done.1 = f32[2,64,32,128]{3,2,1,0:T(8,128)S(1)} collective-permute-done((f32[2,64,32,128]{3,2,1,0:T(8,128)}, f32[2,64,32,128]{3,2,1,0:T(8,128)S(1)}, u32[]{:S(2)}, u32[]{:S(2)}) %collective-permute-start.1) | collective-permute-done | bytes 2097184 | tf_op jit(solution)/shard_map/ppermute | solution.py:261
  276.2 35.2 %all-to-all-done.2 = f32[16,2,8,32,128]{4,3,2,1,0:T(8,128)} async-done(((f32[16,2,8,32,128]{4,3,2,1,0:T(8,128)}), f32[16,2,8,32,128]{4,3,2,1,0:T(8,128)}, u32[]{:S(2)}, u32[]{:S(2)}) %all-to-all-start.2) | async-done | bytes 4194336 | tf_op jit(solution)/shard_map/all_to_all | solution.py:184
  311.4 4.8 all-to-all-start.3
  316.2 10.1 %middle_2.1 = (f32[32,2,128,128]{3,2,1,0:T(8,128)}, f32[32,128,128]{2,1,0:T(8,128)}, f32[2,64,32,128]{3,2,1,0:T(8,128)}, f32[2,64,32,128]{3,2,1,0:T(8,128)}, f32[4,8,128]{2,1,0:T(8,128)}) custom-call(s32[1]{0:T(128)} %bitcast.4.group, f32[256,32,128]{2,1,0:T(8,128)} %bitcast.14.got, bf16[2,256,256]{2,1,0:T(8,128)(2,1)} %pad_maximum_fusion.3.table, ...), custom_call_target="tpu_custom_call" | custom-call | tf_op jit(solution)/shard_map/middle_2/pallas_call | solution.py:215
  333.3 75.4 %all-to-all-done.3 = f32[16,2,8,32,128]{4,3,2,1,0:T(8,128)} async-done(((f32[16,2,8,32,128]{4,3,2,1,0:T(8,128)}), f32[16,2,8,32,128]{4,3,2,1,0:T(8,128)}, u32[]{:S(2)}, u32[]{:S(2)}) %all-to-all-start.3) | async-done | bytes 4194336 | tf_op jit(solution)/shard_map/all_to_all | solution.py:184
  408.7 10.8 %middle_3.1 = (f32[32,2,128,128]{3,2,1,0:T(8,128)}, f32[32,128,128]{2,1,0:T(8,128)}, f32[2,64,32,128]{3,2,1,0:T(8,128)}, f32[2,64,32,128]{3,2,1,0:T(8,128)}, f32[4,8,128]{2,1,0:T(8,128)}) custom-call(s32[1]{0:T(128)} %bitcast.4.group, f32[256,32,128]{2,1,0:T(8,128)} %bitcast.15.got, bf16[2,256,256]{2,1,0:T(8,128)(2,1)} %pad_maximum_fusion.3.table, ...), custom_call_target="tpu_custom_call" | custom-call | tf_op jit(solution)/shard_map/middle_3/pallas_call | solution.py:215
  433.7 17.0 %inverse.1 = f32[256,32,128]{2,1,0:T(8,128)} custom-call(f32[1]{0:T(128)} %bitcast.16.average, f32[32,2,128,128]{3,2,1,0:T(8,128)} %get-tuple-element.44.refs_0_, f32[32,2,128,128]{3,2,1,0:T(8,128)} %get-tuple-element.45.refs_1_, f32[32,2,128,128]{3,2,1,0:T(8,128)} %get-tuple-element.46.refs_2_, f32[32,2,128,128]{3,2,1,0:T(8,128)} %get-tuple-element.47.refs_3_, ...), custom_call_target="tpu_custom_call" | custom-call | tf_op jit(solution)/shard_map/inverse/pallas_call | solution.py:287
  450.6 10.6 %all-to-all-start.4 = ((f32[16,8,2,32,128]{4,3,2,1,0:T(8,128)}), f32[16,8,2,32,128]{4,3,2,1,0:T(8,128)}, u32[]{:S(2)}, u32[]{:S(2)}) async-start(f32[16,8,2,32,128]{4,3,2,1,0:T(8,128)} %bitcast.55), calls=%async_computation.4 | async-start | bytes 8388608 | tf_op jit(solution)/shard_map/all_to_all | solution.py:184
  468.5 39.9 %collective-permute-done.9 = f32[2,64,32,128]{3,2,1,0:T(8,128)S(1)} collective-permute-done((f32[2,64,32,128]{3,2,1,0:T(8,128)}, f32[2,64,32,128]{3,2,1,0:T(8,128)S(1)}, u32[]{:S(2)}, u32[]{:S(2)}) %collective-permute-start.9) | collective-permute-done | bytes 2097184 | tf_op jit(solution)/shard_map/ppermute | solution.py:261
  508.8 3.9 pad_maximum_fusion
  512.7 41.0 %all-to-all-done.4 = f32[16,8,2,32,128]{4,3,2,1,0:T(8,128)} async-done(((f32[16,8,2,32,128]{4,3,2,1,0:T(8,128)}), f32[16,8,2,32,128]{4,3,2,1,0:T(8,128)}, u32[]{:S(2)}, u32[]{:S(2)}) %all-to-all-start.4) | async-done | bytes 4194336 | tf_op jit(solution)/shard_map/all_to_all | solution.py:184
  553.7 4.3 fusion.2
  (89 shorter events, 34.3 us)
Async XLA Ops:
  0.6 121.1 %copy-start = (s32[2,3]{1,0:T(2,128)S(1)}, s32[2,3]{1,0:T(2,128)}, u32[]{:S(2)}) copy-start(s32[2,3]{1,0:T(2,128)} %param.8) | copy-start | bytes 76
  17.9 99.0 %all-to-all-start = ((f32[16,2,8,32,128]{4,3,2,1,0:T(8,128)}), f32[16,2,8,32,128]{4,3,2,1,0:T(8,128)}, u32[]{:S(2)}, u32[]{:S(2)}) async-start(f32[16,2,8,32,128]{4,3,2,1,0:T(8,128)} %forward_0.1.refs_0_), calls=%async_computation | async-start | bytes 8388608 | tf_op jit(solution)/shard_map/all_to_all | solution.py:184
  41.8 82.2 %copy-start.14 = (s32[2,3]{1,0:T(2,128)S(1)}, s32[2,3]{1,0:T(2,128)}, u32[]{:S(2)}) copy-start(s32[2,3]{1,0:T(2,128)} %param.7) | copy-start | bytes 76
  116.9 97.2 %all-to-all-start.1 = ((f32[16,2,8,32,128]{4,3,2,1,0:T(8,128)}), f32[16,2,8,32,128]{4,3,2,1,0:T(8,128)}, u32[]{:S(2)}, u32[]{:S(2)}) async-start(f32[16,2,8,32,128]{4,3,2,1,0:T(8,128)} %forward_1.1.refs_0_), calls=%async_computation.1 | async-start | bytes 8388608 | tf_op jit(solution)/shard_map/all_to_all | solution.py:184
  139.1 47.2 %collective-permute-start = (f32[2,64,32,128]{3,2,1,0:T(8,128)}, f32[2,64,32,128]{3,2,1,0:T(8,128)S(1)}, u32[]{:S(2)}, u32[]{:S(2)}) collective-permute-start(f32[2,64,32,128]{3,2,1,0:T(8,128)} %get-tuple-element.36), channel_id=1, source_target_pairs={{0,16},{16,0},{1,17},{17,1},{2,18},{18,2},{3,19},{19,3},{4,20},{20... | collective-permute-start | bytes 6291464 | tf_op jit(solution)/shard_map/ppermute | solution.py:261
  186.3 27.9 %copy-start.3 = (f32[2,64,32,128]{3,2,1,0:T(8,128)}, f32[2,64,32,128]{3,2,1,0:T(8,128)S(1)}, u32[]{:S(2)}) copy-start(f32[2,64,32,128]{3,2,1,0:T(8,128)S(1)} %collective-permute-done) | copy-start | bytes 6291460
  214.2 97.2 %all-to-all-start.2 = ((f32[16,2,8,32,128]{4,3,2,1,0:T(8,128)}), f32[16,2,8,32,128]{4,3,2,1,0:T(8,128)}, u32[]{:S(2)}, u32[]{:S(2)}) async-start(f32[16,2,8,32,128]{4,3,2,1,0:T(8,128)} %forward_2.1.refs_0_), calls=%async_computation.2 | async-start | bytes 8388608 | tf_op jit(solution)/shard_map/all_to_all | solution.py:184
  229.0 47.2 %collective-permute-start.1 = (f32[2,64,32,128]{3,2,1,0:T(8,128)}, f32[2,64,32,128]{3,2,1,0:T(8,128)S(1)}, u32[]{:S(2)}, u32[]{:S(2)}) collective-permute-start(f32[2,64,32,128]{3,2,1,0:T(8,128)} %get-tuple-element.39), channel_id=1, source_target_pairs={{0,16},{16,0},{1,17},{17,1},{2,18},{18,2},{3,19},{19,3},{4,20},{20... | collective-permute-start | bytes 6291464 | tf_op jit(solution)/shard_map/ppermute | solution.py:261
  276.2 35.2 %copy-start.5 = (f32[2,64,32,128]{3,2,1,0:T(8,128)}, f32[2,64,32,128]{3,2,1,0:T(8,128)S(1)}, u32[]{:S(2)}) copy-start(f32[2,64,32,128]{3,2,1,0:T(8,128)S(1)} %collective-permute-done.1) | copy-start | bytes 6291460
  311.4 97.2 %all-to-all-start.3 = ((f32[16,2,8,32,128]{4,3,2,1,0:T(8,128)}), f32[16,2,8,32,128]{4,3,2,1,0:T(8,128)}, u32[]{:S(2)}, u32[]{:S(2)}) async-start(f32[16,2,8,32,128]{4,3,2,1,0:T(8,128)} %forward_3.1), calls=%async_computation.3 | async-start | bytes 8388608 | tf_op jit(solution)/shard_map/all_to_all | solution.py:184
  326.3 82.4 %collective-permute-start.2 = (f32[2,64,32,128]{3,2,1,0:T(8,128)}, f32[2,64,32,128]{3,2,1,0:T(8,128)S(1)}, u32[]{:S(2)}, u32[]{:S(2)}) collective-permute-start(f32[2,64,32,128]{3,2,1,0:T(8,128)} %get-tuple-element.41), channel_id=1, source_target_pairs={{0,16},{16,0},{1,17},{17,1},{2,18},{18,2},{3,19},{19,3},{4,20},{20... | collective-permute-start | bytes 6291464 | tf_op jit(solution)/shard_map/ppermute | solution.py:261
  408.7 10.8 %copy-start.12 = (f32[4,8,128]{2,1,0:T(8,128)S(1)}, f32[4,8,128]{2,1,0:T(8,128)}, u32[]{:S(2)}) copy-start(f32[4,8,128]{2,1,0:T(8,128)} %get-tuple-element.35.refs_1_) | copy-start | bytes 49156
  408.7 10.8 %copy-start.13 = (f32[4,8,128]{2,1,0:T(8,128)S(1)}, f32[4,8,128]{2,1,0:T(8,128)}, u32[]{:S(2)}) copy-start(f32[4,8,128]{2,1,0:T(8,128)} %get-tuple-element.38) | copy-start | bytes 49156
  420.8 4.4 collective-permute-start.5
  420.8 2.5 collective-permute-start.4
  422.3 1.6 collective-permute-start.3
  426.4 6.7 %collective-permute-start.8 = (f32[]{:T(128)}, f32[]{:T(128)}, u32[]{:S(2)}, u32[]{:S(2)}) collective-permute-start(f32[]{:T(128)} %add.318), channel_id=1, source_target_pairs={{0,12},{1,13},{2,14},{3,15},{4,8},{5,9},{6,10},{7,11},{8,4},{9,5},... | collective-permute-start | bytes 20 | tf_op jit(solution)/shard_map/ppermute | solution.py:147
  428.6 3.3 collective-permute-start.7
  429.3 2.5 collective-permute-start.6
  450.6 13.0 %copy-start.2 = (f32[2,64,32,128]{3,2,1,0:T(8,128)S(1)}, f32[2,64,32,128]{3,2,1,0:T(8,128)}, u32[]{:S(2)}) copy-start(f32[2,64,32,128]{3,2,1,0:T(8,128)} %get-tuple-element.52) | copy-start | bytes 6291460
  450.6 103.1 %all-to-all-start.4 = ((f32[16,8,2,32,128]{4,3,2,1,0:T(8,128)}), f32[16,8,2,32,128]{4,3,2,1,0:T(8,128)}, u32[]{:S(2)}, u32[]{:S(2)}) async-start(f32[16,8,2,32,128]{4,3,2,1,0:T(8,128)} %bitcast.55), calls=%async_computation.4 | async-start | bytes 8388608 | tf_op jit(solution)/shard_map/all_to_all | solution.py:184
  461.2 47.1 %collective-permute-start.9 = (f32[2,64,32,128]{3,2,1,0:T(8,128)}, f32[2,64,32,128]{3,2,1,0:T(8,128)S(1)}, u32[]{:S(2)}, u32[]{:S(2)}) collective-permute-start(f32[2,64,32,128]{3,2,1,0:T(8,128)} %get-tuple-element.59), channel_id=1, source_target_pairs={{0,16},{16,0},{1,17},{17,1},{2,18},{18,2},{3,19},{19,3},{4,20},{20... | collective-permute-start | bytes 6291464 | tf_op jit(solution)/shard_map/ppermute | solution.py:261
  466.3 42.0 %copy-start.10 = (f32[2,64,32,128]{3,2,1,0:T(8,128)S(1)}, f32[2,64,32,128]{3,2,1,0:T(8,128)}, u32[]{:S(2)}) copy-start(f32[2,64,32,128]{3,2,1,0:T(8,128)} %get-tuple-element.58) | copy-start | bytes 6291460
  508.8 49.2 %copy-start.1 = (s32[2,3]{1,0:T(2,128)S(1)}, s32[2,3]{1,0:T(2,128)}, u32[]{:S(2)}) copy-start(s32[2,3]{1,0:T(2,128)} %param.8) | copy-start | bytes 76
  (6 other events, 34.6 us)

commit v2 on v1

--- a/solution.py
+++ b/solution.py
@@ -10,6 +10,7 @@
 from jax.experimental.pallas import tpu as pltpu
 from jax.sharding import PartitionSpec as P
 
+
 CROP = 128
 LANES = 128
 ROWS = 8
@@ -55,25 +56,31 @@
     )
 
 
-def forward_kernel(frame, table_x, table_y, *refs):
-    out = refs[-1]
+def forward_kernel(device, frame, table_x, table_y, *refs, partners):
+    outs, scratch = refs[-1 - partners : -1], refs[-1]
     count, ny, nx = frame.shape
-    devices, _, _, rows, _ = out.shape
+    rows = outs[0].shape[2]
     column = [jnp.concatenate([table_x[i, :nx, :], table_x[i, nx:, :]], 1) for i in range(2)]
     for z in range(count):
         plane = parts(dot3(parts(frame[z]), column))
         both = dot3((table_y[0], table_y[1]), plane)
-        real = both[:ny, :LANES] - both[ny:, LANES:]
-        imag = -both[:ny, LANES:] - both[ny:, :LANES]
-        out[:, 0, z] = real.reshape(devices, rows, LANES)
-        out[:, 1, z] = imag.reshape(devices, rows, LANES)
-
-
-def middle_kernel(group, got, table, ref_own, ref_far, turn_z, turn_yx, cross, size, own, far, sums):
+        scratch[z, 0] = both[:ny, :LANES] - both[ny:, LANES:]
+        scratch[z, 1] = -both[:ny, LANES:] - both[ny:, :LANES]
+    for k, out in enumerate(outs):
+        at = pl.ds(pl.multiple_of((device[0] ^ k) * rows, rows), rows)
+        for z in range(count):
+            out[0, z] = scratch[z, 0, at, :]
+            out[1, z] = scratch[z, 1, at, :]
+
+
+def middle_kernel(group, *refs, partners, after):
     del group
+    refs = refs[:partners] + refs[partners + after :]
+    gots, (table, ref_own, ref_far, turn_z, turn_yx, cross, size, own, far, sums) = refs[:-10], refs[-10:]
+    each = gots[0].shape[0]
     nz = cross.shape[2]
     half = own.shape[1]
-    flat = got.reshape(2 * nz * ROWS, LANES)
+    flats = [got.reshape(each * ROWS, LANES) for got in gots]
     near = ref_own.reshape(2 * half * ROWS, LANES)
     away = ref_far.reshape(2 * half * ROWS, LANES)
     own_flat = own.reshape(2 * half * ROWS, LANES)
@@ -82,7 +89,10 @@
     zc, zs = turn_z[0], turn_z[1]
     total = jnp.zeros((8, LANES), F32)
     for pair in range(0, ROWS, 2):
-        taken = [flat[pl.ds(r, 2 * nz, stride=ROWS), :] for r in (pair, pair + 1)]
+        taken = [
+            jnp.concatenate([flat[pl.ds(r, each, stride=ROWS), :] for flat in flats], 0)
+            for r in (pair, pair + 1)
+        ]
         freq = dot3(matrix, parts(jnp.concatenate(taken, 1)))
         for r in (pair, pair + 1):
             at = slice((r - pair) * LANES, (r - pair + 1) * LANES)
@@ -108,12 +118,14 @@
     sums[0] = total
 
 
-def inverse_kernel(average, *refs):
-    table_x, table_z, out = refs[-3:]
-    crosses, sizes = refs[: len(refs) // 2 - 1], refs[len(refs) // 2 - 1 : -3]
+def inverse_kernel(average, *refs, chunks):
+    crosses, sizes = refs[:chunks], refs[chunks : 2 * chunks]
+    table_x, table_z = refs[2 * chunks : 2 * chunks + 2]
+    outs = refs[2 * chunks + 2 :]
+    each = outs[0].shape[0]
     nz = crosses[0].shape[2]
     mean = average[0]
-    flat = out.reshape(2 * CROP * ROWS, LANES)
+    flats = [out.reshape(each * ROWS, LANES) for out in outs]
     matrix = (table_z[0], table_z[1])
     width = None
     for c, (cross, size) in enumerate(zip(crosses, sizes)):
@@ -133,8 +145,35 @@
             1,
         )
         depth = dot3(matrix, parts(stacked))
-        flat[pl.ds(pair, 2 * CROP, stride=ROWS), :] = depth[:, :CROP]
-        flat[pl.ds(pair + 1, 2 * CROP, stride=ROWS), :] = depth[:, CROP:]
+        for k, flat in enumerate(flats):
+            at = slice(k * each, (k + 1) * each)
+            flat[pl.ds(pair, each, stride=ROWS), :] = depth[at, :CROP]
+            flat[pl.ds(pair + 1, each, stride=ROWS), :] = depth[at, CROP:]
+
+
+def partial_kernel(table, *refs, near):
+    slabs, out = refs[:near], refs[-1]
+    planes = out.shape[1]
+    matrix = (table[0], table[1])
+    for z in range(0, planes, 2):
+        stacked = jnp.concatenate(
+            [
+                jnp.concatenate(
+                    [slab[2 * y : 2 * y + 2].reshape(-1, CROP) for slab in slabs], 0
+                )
+                for y in (z, min(z + 1, planes - 1))
+            ],
+            1,
+        )
+        both = dot3(matrix, parts(stacked))
+        out[0, z] = both[:, :CROP]
+        if z + 1 < planes:
+            out[0, z + 1] = both[:, CROP:]
+
+
+def mark_kernel(after, out):
+    del after
+    out[...] = jnp.zeros(out.shape, F32)
 
 
 def total_over(value, axis, size):
@@ -142,10 +181,8 @@
         return lax.psum(value, axis)
     step = 1
     while step < size:
-        flips = (1, 2, 3) if 2 * step < size else (1,)
-        pairs = [[(i, i ^ (flip * step)) for i in range(size)] for flip in flips]
-        value = value + sum(lax.ppermute(value, axis, pair) for pair in pairs)
-        step *= len(flips) + 1
+        value = value + lax.ppermute(value, axis, [(i, i ^ step) for i in range(size)])
+        step *= 2
     return value
 
 
@@ -167,29 +204,45 @@
 
     def send(c, *after):
         return pl.pallas_call(
-            forward_kernel,
-            grid=(planes // 2,),
-            in_specs=[
-                pl.BlockSpec((2, ny, nx), lambda z: (z, 0, 0)),
-                pl.BlockSpec((2, 2 * nx, LANES), lambda z: (0, 0, c)),
-                whole((2, 2 * ny, ny)),
-            ]
-            + [pl.BlockSpec(memory_space=pl.ANY)] * len(after),
-            out_specs=pl.BlockSpec((devices, 2, 2, rows, LANES), lambda z: (0, 0, z, 0, 0)),
-            out_shape=jax.ShapeDtypeStruct((devices, 2, planes, rows, LANES), F32),
-            name=f"forward_{c}",
-        )(frame, table_x, table_y, *after)
-
-    def exchange(packed):
-        return lax.all_to_all(packed, "dev", split_axis=0, concat_axis=0, tiled=True)
-
+            functools.partial(forward_kernel, partners=devices),
+            grid_spec=pltpu.PrefetchScalarGridSpec(
+                num_scalar_prefetch=1,
+                grid=(planes // 2,),
+                in_specs=[
+                    pl.BlockSpec((2, ny, nx), lambda z, d: (z, 0, 0)),
+                    pl.BlockSpec((2, 2 * nx, LANES), lambda z, d: (0, 0, c)),
+                    whole((2, 2 * ny, ny)),
+                ]
+                + [pl.BlockSpec(memory_space=pl.ANY)] * len(after),
+                out_specs=[pl.BlockSpec((2, 2, rows, LANES), lambda z, d: (0, z, 0, 0))] * devices,
+                scratch_shapes=[pltpu.VMEM((2, 2, ny, LANES), F32)],
+            ),
+            out_shape=[jax.ShapeDtypeStruct((2, planes, rows, LANES), F32)] * devices,
+        )(device_number, frame, table_x, table_y, *after)
+
+    def exchange(pieces):
+        got = list(pieces)
+        for k in sorted(range(1, devices), reverse=True):
+            got[k] = lax.ppermute(pieces[k], "dev", [(i, i ^ k) for i in range(devices)])
+        return got
+
+    def mark(after):
+        return pl.pallas_call(
+            mark_kernel,
+            in_specs=[pl.BlockSpec(memory_space=pl.ANY)],
+            out_shape=jax.ShapeDtypeStruct((8, LANES), F32),
+        )(after)
+
+    partner = device ^ ints(devices)
+    device_number = device.astype(jnp.int32).reshape(1)
     first = send(0)
     shifts, offsets, first = lax.optimization_barrier((shifts, offsets, first))
+    order = (partner[:, None] * planes + ints(planes)).reshape(-1)
     drift = lax.dynamic_index_in_dim(shifts, group, 0, keepdims=False)
     corner = lax.dynamic_index_in_dim(offsets, group, 0, keepdims=False)
     kz = (ints(nz) + group * half) % nz
     ky = device * rows + ints(rows)
-    cos_z, sin_z = wave(kz, ints(nz), nz)
+    cos_z, sin_z = wave(kz, order, nz)
     split = lambda table: table.reshape(nz, devices, planes)
     table_z = halves(
         factor
@@ -211,14 +264,18 @@
     group_number = group.astype(jnp.int32).reshape(1)
     steps = rows // ROWS
 
-    def middle(got, c):
+    def middle(gots, c, *after):
         return pl.pallas_call(
-            middle_kernel,
+            functools.partial(middle_kernel, partners=devices, after=len(after)),
             grid_spec=pltpu.PrefetchScalarGridSpec(
                 num_scalar_prefetch=1,
                 grid=(steps,),
                 in_specs=[
-                    pl.BlockSpec((2 * nz, ROWS, LANES), lambda i, g: (0, i, 0)),
+                    pl.BlockSpec((2 * planes, ROWS, LANES), lambda i, g: (0, i, 0)),
+                ]
+                * devices
+                + [pl.BlockSpec(memory_space=pl.ANY)] * len(after)
+                + [
                     whole((2, 2 * nz, 2 * nz)),
                     pl.BlockSpec((2, 1, half, ROWS, LANES), lambda i, g: (0, g[0], 0, i, c)),
                     pl.BlockSpec((2, 1, half, ROWS, LANES), lambda i, g: (0, groups - 1 - g[0], 0, i, c)),
@@ -240,21 +297,19 @@
                 jax.ShapeDtypeStruct((2, half, rows, LANES), F32),
                 jax.ShapeDtypeStruct((steps, 8, LANES), F32),
             ],
-            name=f"middle_{c}",
-        )(group_number, got, table_z, ref_view, ref_view, turn_z, turn_yx)
+        )(group_number, *gots, *after, table_z, ref_view, ref_view, turn_z, turn_yx)
 
     crosses, sizes, owns, fars, sums = [], [], [], [], []
     swap = [(i, groups - 1 - i) for i in range(groups)]
     packed = [first]
     for c in range(chunks):
         if c + 1 < chunks:
-            packed.append(send(c + 1, packed[c], *sums[-1:]))
-        if c > 1:
-            packed[c], fars[c - 2] = lax.optimization_barrier((packed[c], fars[c - 2]))
-        got = exchange(packed[c]).reshape(2 * nz, rows, LANES)
-        if c > 0 and c == chunks - 1:
-            got, fars[c - 1] = lax.optimization_barrier((got, fars[c - 1]))
-        cross, size, own, far, part = middle(got, c)
+            packed.append(send(c + 1, packed[c][0], *sums[-1:]))
+        gots = [got.reshape(2 * planes, rows, LANES) for got in exchange(packed[c])]
+        marks = [mark(packed[c + 1][0])] if c + 1 < chunks else []
+        if 0 < c < chunks - 1:
+            gots[0], fars[c - 1] = lax.optimization_barrier((gots[0], fars[c - 1]))
+        cross, size, own, far, part = middle(gots, c, *marks)
         sizes.append(size)
         crosses.append(cross)
         owns.append(own)
@@ -274,30 +329,66 @@
             [jnp.concatenate([cb, sb], 2), jnp.concatenate([-sb, cb], 2)], 1
         ).reshape(2 * nx, 2 * CROP)
     )
+    leaf = CROP // devices
+    near = 1 << ((devices.bit_length() - 1) // 2)
+    far_count = devices // near
+    splits = 2 if leaf % 2 == 0 else 1
+    part = leaf // splits
+    turn = (ints(far_count)[None, :] * near) ^ ints(near)[:, None]
+    turn = (device ^ turn).reshape(1, near, far_count, 1)
+    here = ints(splits).reshape(-1, 1, 1, 1) * part + ints(part).reshape(1, 1, 1, -1)
+    take_z = (turn * leaf + here + corner[0]).reshape(-1) % nz
     bz, dz = wave(take_z, kz, nz)
     back_z = halves(
         jnp.stack(
             [jnp.concatenate([bz, -dz], 1), jnp.concatenate([dz, bz], 1)], 1
         ).reshape(2 * CROP, 2 * nz)
     )
-    cos_b, sin_b = wave(take_y, ints(ny), ny)
-    back_y = factor * jnp.stack(
-        [cos_b.reshape(CROP, devices, rows), -sin_b.reshape(CROP, devices, rows)], 2
-    )
+    rows_there = ((device ^ ints(near))[:, None] * rows + ints(rows)).reshape(-1)
+    cos_b, sin_b = wave(take_y, rows_there, ny)
+    cos_b, sin_b = cos_b.reshape(CROP, near, rows), sin_b.reshape(CROP, near, rows)
+    back_y = halves(factor * jnp.stack([cos_b, -sin_b], 2)).reshape(2, CROP, -1)
+    lot = 2 * far_count * part
+
     back = pl.pallas_call(
-        inverse_kernel,
+        functools.partial(inverse_kernel, chunks=chunks),
         grid=(steps,),
         in_specs=[pl.BlockSpec(memory_space=pltpu.SMEM)]
         + [pl.BlockSpec((ROWS, 2, nz, LANES), lambda i: (i, 0, 0, 0))] * chunks
         + [pl.BlockSpec((ROWS, nz, LANES), lambda i: (i, 0, 0))] * chunks
         + [whole((2, 2 * nx, 2 * CROP)), whole((2, 2 * CROP, 2 * nz))],
-        out_specs=pl.BlockSpec((2 * CROP, ROWS, LANES), lambda i: (0, i, 0)),
-        out_shape=jax.ShapeDtypeStruct((2 * CROP, rows, LANES), F32),
-        name="inverse",
+        out_specs=[pl.BlockSpec((lot, ROWS, LANES), lambda i: (0, i, 0))] * (splits * near),
+        out_shape=[jax.ShapeDtypeStruct((lot, rows, LANES), F32)] * (splits * near),
     )(average.reshape(1), *crosses, *sizes, back_x, back_z)
-    slab = exchange(back.reshape(devices, CROP // devices, 2, rows, CROP))
-    field = jnp.einsum("szprx,yspr->zyx", slab, back_y, precision=lax.Precision.HIGH)
+
+    def partial(slabs, *after):
+        return pl.pallas_call(
+            functools.partial(partial_kernel, near=near),
+            grid=(far_count,),
+            in_specs=[whole(back_y.shape)]
+            + [pl.BlockSpec((2 * part, rows, CROP), lambda f: (f, 0, 0))] * near
+            + [pl.BlockSpec(memory_space=pl.ANY)] * len(after),
+            out_specs=pl.BlockSpec((1, part, CROP, CROP), lambda f: (f, 0, 0, 0)),
+            out_shape=jax.ShapeDtypeStruct((far_count, part, CROP, CROP), F32),
+        )(back_y, *slabs, *after)
+
     new_reference = jnp.concatenate([own + far for own, far in zip(owns, fars)], 3)
+    gathered = []
+    for h in range(splits):
+        slabs = list(back[h * near : (h + 1) * near])
+        for k in range(1, near):
+            slabs[k] = lax.ppermute(slabs[k], "dev", [(i, i ^ k) for i in range(devices)])
+        gathered.append(slabs)
+    fields = []
+    for h in range(splits):
+        sums_y = partial(gathered[h], *([new_reference] if h else []))
+        field = sums_y[0]
+        moved = [
+            lax.ppermute(sums_y[k], "dev", [(i, i ^ (k * near)) for i in range(devices)])
+            for k in range(1, far_count)
+        ]
+        fields.append(field + sum(moved))
+    field = jnp.concatenate(fields, 0)
     return (field[None], new_reference)
 
 

time: 559 us -> 613 us (1.097)
  starting transfers between devices: 43.6 us -> 124 us
  waiting for transfers between devices: 353 us -> 304 us
  Pallas kernels: 127 us -> 141 us
  other arithmetic: 20 us -> 30.5 us
    ppermute x6 -> x76, waiting for transfers between devices: 1.49 us -> 304 us  [the longest x60 261 us: exchange(): lax.ppermute(pieces[k], 'dev', [(i, i ^ k) for i in range(devices)])]
    all_to_all x5 -> x0, waiting for transfers between devices: 255 us -> none  [exchange(): lax.all_to_all(packed, 'dev', split_axis=0, concat_axis=0, tiled=True)]
    ppermute x6 -> x76, starting transfers between devices: 7.02 us -> 119 us  [the longest x60 97.2 us: exchange(): lax.ppermute(pieces[k], 'dev', [(i, i ^ k) for i in range(devices)])]
    ppermute x4, waiting for transfers between devices: 97 us -> 0.01 us  [local(): fars.append(lax.ppermute(far, 'grp', swap))]
    all_to_all x5 -> x0, starting transfers between devices: 31.5 us -> none  [exchange(): lax.all_to_all(packed, 'dev', split_axis=0, concat_axis=0, tiled=True)]
    pallas_call x9 -> x14, Pallas kernels: 127 us -> 141 us  [the longest x4 71.8 us: send(): pl.pallas_call(functools.partial(forward_kernel, partners=devices), grid_...]
    add x4, other arithmetic: 3.54 us -> 10.7 us  [local(): own + far]
  transfers between devices with their start and end apart: 15 -> 80, of which waited for: 11 -> 44; matrix products, arithmetic and copies ran while one was open for 4% -> 6% of each run, Pallas kernels for 15% -> 18%
where the time goes in v2:
time: 613 us; the launch traced here: 612 us
  waiting for transfers between devices  304 us (50%)
  Pallas kernels  141 us (23%)
  starting transfers between devices  124 us (20%)
  other arithmetic  30.5 us (5%)
  local copies, waits for them, and re-layouts  8.52 us (1%)
    ppermute x60, waiting for transfers between devices, exchange(): lax.ppermute(pieces[k], 'dev', [(i, i ^ k) for i in range(devices)])  261 us
    ppermute x60, starting transfers between devices, exchange(): lax.ppermute(pieces[k], 'dev', [(i, i ^ k) for i in range(devices)])  97.2 us
    pallas_call x4, Pallas kernels, send(): pl.pallas_call(functools.partial(forward_kernel, partners=devices), grid_...  71.8 us
    pallas_call x4, Pallas kernels, middle(): pl.pallas_call(functools.partial(middle_kernel, partners=devices, after=l...  41.9 us
    ppermute x6, waiting for transfers between devices, local(): lax.ppermute(sums_y[k], 'dev', [(i, i ^ k * near) for i in range(devices)])  22.3 us
    pallas_call x1, Pallas kernels, local(): pl.pallas_call(functools.partial(inverse_kernel, chunks=chunks), grid=(st...  16.8 us
    ppermute x6, waiting for transfers between devices, local(): lax.ppermute(slabs[k], 'dev', [(i, i ^ k) for i in range(devices)])  15.6 us
  transfers between devices with their start and end apart: 80, of which 44 were waited for; matrix products, arithmetic and copies ran while one was open for 6% of the time, Pallas kernels for 18%

profile of v2, /device:TPU:13, one launch (start us, length us, event | category | flops | bytes accessed | tf_op | source)
XLA Modules:
  0.0 611.8 jit_solution(10848201645999768653)
XLA Ops:
  0.7 17.9 %shard_map.68 = (f32[2,8,32,128]{3,2,1,0:T(8,128)}, f32[2,8,32,128]{3,2,1,0:T(8,128)}, f32[2,8,32,128]{3,2,1,0:T(8,128)}, f32[2,8,32,128]{3,2,1,0:T(8,128)}, f32...) custom-call(s32[1]{0:T(128)} %bitcast.device, ...), custom_call_target="tpu_custom_call" | custom-call | tf_op jit(solution)/shard_map/pallas_call | solution.py:206
  39.6 9.8 %collective-permute-done.5 = f32[2,8,32,128]{3,2,1,0:T(8,128)S(1)} collective-permute-done((f32[2,8,32,128]{3,2,1,0:T(8,128)}, f32[2,8,32,128]{3,2,1,0:T(8,128)S(1)}, u32[]{:S(2)}, u32[]{:S(2)}) %collective-permute-start.5) | collective-permute-done | bytes 262176 | tf_op jit(solution)/shard_map/ppermute | solution.py:226
  57.7 23.5 %collective-permute-done.8 = f32[2,8,32,128]{3,2,1,0:T(8,128)S(1)} collective-permute-done((f32[2,8,32,128]{3,2,1,0:T(8,128)}, f32[2,8,32,128]{3,2,1,0:T(8,128)S(1)}, u32[]{:S(2)}, u32[]{:S(2)}) %collective-permute-start.8) | collective-permute-done | bytes 262176 | tf_op jit(solution)/shard_map/ppermute | solution.py:226
  81.2 11.1 %collective-permute-done.9 = f32[2,8,32,128]{3,2,1,0:T(8,128)S(1)} collective-permute-done((f32[2,8,32,128]{3,2,1,0:T(8,128)}, f32[2,8,32,128]{3,2,1,0:T(8,128)S(1)}, u32[]{:S(2)}, u32[]{:S(2)}) %collective-permute-start.9) | collective-permute-done | bytes 262176 | tf_op jit(solution)/shard_map/ppermute | solution.py:226
  93.1 17.9 %shard_map.69 = (f32[2,8,32,128]{3,2,1,0:T(8,128)}, f32[2,8,32,128]{3,2,1,0:T(8,128)}, f32[2,8,32,128]{3,2,1,0:T(8,128)}, f32[2,8,32,128]{3,2,1,0:T(8,128)}, f32...) custom-call(s32[1]{0:T(128)} %bitcast.device, ...), custom_call_target="tpu_custom_call" | custom-call | tf_op jit(solution)/shard_map/pallas_call | solution.py:206
  126.9 10.4 %shard_map.71 = (f32[32,2,128,128]{3,2,1,0:T(8,128)}, f32[32,128,128]{2,1,0:T(8,128)}, f32[2,64,32,128]{3,2,1,0:T(8,128)}, f32[2,64,32,128]{3,2,1,0:T(8,128)}, f32[4,8,128]{2,1,0:T(8,128)}) custom-call(s32[1]{0:T(128)} %bitcast.4.group, f32[16,32,128]{2,1,0:T(8,128)} %bitcast.128, f32[16,32,128]{2,1,0:T(8,128)} %bitcast.138, f32[16,32,128]{2,1,0:T(8,128)} %bitcast.139, ...), custom_call_target="tpu_custom_call" | custom-call | tf_op jit(solution)/shard_map/pallas_call | solution.py:268
  158.3 10.3 %collective-permute-done.21 = f32[2,8,32,128]{3,2,1,0:T(8,128)} collective-permute-done((f32[2,8,32,128]{3,2,1,0:T(8,128)}, f32[2,8,32,128]{3,2,1,0:T(8,128)}, u32[]{:S(2)}, u32[]{:S(2)}) %collective-permute-start.21) | collective-permute-done | bytes 262176 | tf_op jit(solution)/shard_map/ppermute | solution.py:226
  178.9 17.8 %collective-permute-done.24 = f32[2,8,32,128]{3,2,1,0:T(8,128)} collective-permute-done((f32[2,8,32,128]{3,2,1,0:T(8,128)}, f32[2,8,32,128]{3,2,1,0:T(8,128)}, u32[]{:S(2)}, u32[]{:S(2)}) %collective-permute-start.24) | collective-permute-done | bytes 262176 | tf_op jit(solution)/shard_map/ppermute | solution.py:226
  198.2 9.6 %collective-permute-done.25 = f32[2,8,32,128]{3,2,1,0:T(8,128)} collective-permute-done((f32[2,8,32,128]{3,2,1,0:T(8,128)}, f32[2,8,32,128]{3,2,1,0:T(8,128)}, u32[]{:S(2)}, u32[]{:S(2)}) %collective-permute-start.25) | collective-permute-done | bytes 262176 | tf_op jit(solution)/shard_map/ppermute | solution.py:226
  220.7 18.0 %shard_map.72 = (f32[2,8,32,128]{3,2,1,0:T(8,128)}, f32[2,8,32,128]{3,2,1,0:T(8,128)}, f32[2,8,32,128]{3,2,1,0:T(8,128)}, f32[2,8,32,128]{3,2,1,0:T(8,128)}, f32...) custom-call(s32[1]{0:T(128)} %bitcast.device, ...), custom_call_target="tpu_custom_call" | custom-call | tf_op jit(solution)/shard_map/pallas_call | solution.py:206
  248.5 10.5 %shard_map.74 = (f32[32,2,128,128]{3,2,1,0:T(8,128)}, f32[32,128,128]{2,1,0:T(8,128)}, f32[2,64,32,128]{3,2,1,0:T(8,128)}, f32[2,64,32,128]{3,2,1,0:T(8,128)}, f32[4,8,128]{2,1,0:T(8,128)}) custom-call(s32[1]{0:T(128)} %bitcast.4.group, f32[16,32,128]{2,1,0:T(8,128)} %bitcast.127, f32[16,32,128]{2,1,0:T(8,128)} %bitcast.146, f32[16,32,128]{2,1,0:T(8,128)} %bitcast.147, ...), custom_call_target="tpu_custom_call" | custom-call | tf_op jit(solution)/shard_map/pallas_call | solution.py:268
  263.7 17.9 %shard_map.75 = (f32[2,8,32,128]{3,2,1,0:T(8,128)}, f32[2,8,32,128]{3,2,1,0:T(8,128)}, f32[2,8,32,128]{3,2,1,0:T(8,128)}, f32[2,8,32,128]{3,2,1,0:T(8,128)}, f32...) custom-call(s32[1]{0:T(128)} %bitcast.device, ...), custom_call_target="tpu_custom_call" | custom-call | tf_op jit(solution)/shard_map/pallas_call | solution.py:206
  301.7 11.3 %collective-permute-done.52 = f32[2,8,32,128]{3,2,1,0:T(8,128)} collective-permute-done((f32[2,8,32,128]{3,2,1,0:T(8,128)}, f32[2,8,32,128]{3,2,1,0:T(8,128)}, u32[]{:S(2)}, u32[]{:S(2)}) %collective-permute-start.52) | collective-permute-done | bytes 262176 | tf_op jit(solution)/shard_map/ppermute | solution.py:226
  324.8 18.8 %collective-permute-done.55 = f32[2,8,32,128]{3,2,1,0:T(8,128)} collective-permute-done((f32[2,8,32,128]{3,2,1,0:T(8,128)}, f32[2,8,32,128]{3,2,1,0:T(8,128)}, u32[]{:S(2)}, u32[]{:S(2)}) %collective-permute-start.55) | collective-permute-done | bytes 262176 | tf_op jit(solution)/shard_map/ppermute | solution.py:226
  354.9 14.0 %collective-permute-done.58 = f32[2,8,32,128]{3,2,1,0:T(8,128)} collective-permute-done((f32[2,8,32,128]{3,2,1,0:T(8,128)}, f32[2,8,32,128]{3,2,1,0:T(8,128)}, u32[]{:S(2)}, u32[]{:S(2)}) %collective-permute-start.58) | collective-permute-done | bytes 262176 | tf_op jit(solution)/shard_map/ppermute | solution.py:226
  369.0 14.8 %collective-permute-start.61 = (f32[2,8,32,128]{3,2,1,0:T(8,128)}, f32[2,8,32,128]{3,2,1,0:T(8,128)S(1)}, u32[]{:S(2)}, u32[]{:S(2)}) collective-permute-start(f32[2,8,32,128]{3,2,1,0:T(8,128)} %get-tuple-element.204), channel_id=1, source_target_pairs={{0,15},{1,14},{2,13},{3,12},{4,11},{5,10},{6,9},{7,8},{8,7},{9,6},... | collective-permute-start | bytes 786440 | tf_op jit(solution)/shard_map/ppermute | solution.py:226
  391.1 11.3 %collective-permute-done.60 = f32[2,8,32,128]{3,2,1,0:T(8,128)S(1)} collective-permute-done((f32[2,8,32,128]{3,2,1,0:T(8,128)}, f32[2,8,32,128]{3,2,1,0:T(8,128)S(1)}, u32[]{:S(2)}, u32[]{:S(2)}) %collective-permute-start.60) | collective-permute-done | bytes 262176 | tf_op jit(solution)/shard_map/ppermute | solution.py:226
  402.3 11.2 %collective-permute-done.61 = f32[2,8,32,128]{3,2,1,0:T(8,128)S(1)} collective-permute-done((f32[2,8,32,128]{3,2,1,0:T(8,128)}, f32[2,8,32,128]{3,2,1,0:T(8,128)S(1)}, u32[]{:S(2)}, u32[]{:S(2)}) %collective-permute-start.61) | collective-permute-done | bytes 262176 | tf_op jit(solution)/shard_map/ppermute | solution.py:226
  414.7 10.5 %shard_map.78 = (f32[32,2,128,128]{3,2,1,0:T(8,128)}, f32[32,128,128]{2,1,0:T(8,128)}, f32[2,64,32,128]{3,2,1,0:T(8,128)}, f32[2,64,32,128]{3,2,1,0:T(8,128)}, f32[4,8,128]{2,1,0:T(8,128)}) custom-call(s32[1]{0:T(128)} %bitcast.4.group, f32[16,32,128]{2,1,0:T(8,128)} %bitcast.129, f32[16,32,128]{2,1,0:T(8,128)} %bitcast.143, f32[16,32,128]{2,1,0:T(8,128)} %bitcast.144, ...), custom_call_target="tpu_custom_call" | custom-call | tf_op jit(solution)/shard_map/pallas_call | solution.py:268
  430.2 14.6 %collective-permute-done.42 = f32[2,8,32,128]{3,2,1,0:T(8,128)} collective-permute-done((f32[2,8,32,128]{3,2,1,0:T(8,128)}, f32[2,8,32,128]{3,2,1,0:T(8,128)}, u32[]{:S(2)}, u32[]{:S(2)}) %collective-permute-start.42) | collective-permute-done | bytes 262176 | tf_op jit(solution)/shard_map/ppermute | solution.py:226
  452.9 17.0 %collective-permute-done.44 = f32[2,8,32,128]{3,2,1,0:T(8,128)} collective-permute-done((f32[2,8,32,128]{3,2,1,0:T(8,128)}, f32[2,8,32,128]{3,2,1,0:T(8,128)}, u32[]{:S(2)}, u32[]{:S(2)}) %collective-permute-start.44) | collective-permute-done | bytes 262176 | tf_op jit(solution)/shard_map/ppermute | solution.py:226
  481.1 10.5 %shard_map.77 = (f32[32,2,128,128]{3,2,1,0:T(8,128)}, f32[32,128,128]{2,1,0:T(8,128)}, f32[2,64,32,128]{3,2,1,0:T(8,128)}, f32[2,64,32,128]{3,2,1,0:T(8,128)}, f32[4,8,128]{2,1,0:T(8,128)}) custom-call(s32[1]{0:T(128)} %bitcast.4.group, f32[16,32,128]{2,1,0:T(8,128)} %bitcast.126, f32[16,32,128]{2,1,0:T(8,128)} %bitcast.133, f32[16,32,128]{2,1,0:T(8,128)} %bitcast.134, ...), custom_call_target="tpu_custom_call" | custom-call | tf_op jit(solution)/shard_map/pallas_call | solution.py:268
  509.5 16.8 %shard_map.79 = (f32[32,32,128]{2,1,0:T(8,128)}, f32[32,32,128]{2,1,0:T(8,128)}, f32[32,32,128]{2,1,0:T(8,128)}, f32[32,32,128]{2,1,0:T(8,128)}, f32[32,32,128]{...) custom-call(f32[1]{0:T(128)} %bitcast.76.average, ...), custom_call_target="tpu_custom_call" | custom-call | tf_op jit(solution)/shard_map/pallas_call | solution.py:353
  586.6 12.2 %collective-permute-done.71 = f32[4,128,128]{2,1,0:T(8,128)S(1)} collective-permute-done((f32[4,128,128]{2,1,0:T(8,128)}, f32[4,128,128]{2,1,0:T(8,128)S(1)}, u32[]{:S(2)}, u32[]{:S(2)}) %collective-permute-start.71) | collective-permute-done | bytes 262176 | tf_op jit(solution)/shard_map/ppermute | solution.py:387
  (300 shorter events, 269.5 us)
Async XLA Ops:
  35.7 45.5 %collective-permute-start.8 = (f32[2,8,32,128]{3,2,1,0:T(8,128)}, f32[2,8,32,128]{3,2,1,0:T(8,128)S(1)}, u32[]{:S(2)}, u32[]{:S(2)}) collective-permute-start(f32[2,8,32,128]{3,2,1,0:T(8,128)} %get-tuple-element.142), channel_id=1, source_target_pairs={{0,9},{1,8},{2,11},{3,10},{4,13},{5,12},{6,15},{7,14},{8,1},{9,0},... | collective-permute-start | bytes 786440 | tf_op jit(solution)/shard_map/ppermute | solution.py:226
  35.8 56.5 %collective-permute-start.9 = (f32[2,8,32,128]{3,2,1,0:T(8,128)}, f32[2,8,32,128]{3,2,1,0:T(8,128)S(1)}, u32[]{:S(2)}, u32[]{:S(2)}) collective-permute-start(f32[2,8,32,128]{3,2,1,0:T(8,128)} %get-tuple-element.143), channel_id=1, source_target_pairs={{0,10},{1,11},{2,8},{3,9},{4,14},{5,15},{6,12},{7,13},{8,2},{9,3},... | collective-permute-start | bytes 786440 | tf_op jit(solution)/shard_map/ppermute | solution.py:226
  49.4 63.7 %collective-permute-start.10 = (f32[2,8,32,128]{3,2,1,0:T(8,128)}, f32[2,8,32,128]{3,2,1,0:T(8,128)S(1)}, u32[]{:S(2)}, u32[]{:S(2)}) collective-permute-start(f32[2,8,32,128]{3,2,1,0:T(8,128)} %get-tuple-element.144), channel_id=1, source_target_pairs={{0,11},{1,10},{2,9},{3,8},{4,15},{5,14},{6,13},{7,12},{8,3},{9,2},... | collective-permute-start | bytes 786440 | tf_op jit(solution)/shard_map/ppermute | solution.py:226
  55.0 58.1 %collective-permute-start.11 = (f32[2,8,32,128]{3,2,1,0:T(8,128)}, f32[2,8,32,128]{3,2,1,0:T(8,128)S(1)}, u32[]{:S(2)}, u32[]{:S(2)}) collective-permute-start(f32[2,8,32,128]{3,2,1,0:T(8,128)} %get-tuple-element.145), channel_id=1, source_target_pairs={{0,12},{1,13},{2,14},{3,15},{4,8},{5,9},{6,10},{7,11},{8,4},{9,5},... | collective-permute-start | bytes 786440 | tf_op jit(solution)/shard_map/ppermute | solution.py:226
  55.2 59.8 %collective-permute-start.12 = (f32[2,8,32,128]{3,2,1,0:T(8,128)}, f32[2,8,32,128]{3,2,1,0:T(8,128)}, u32[]{:S(2)}, u32[]{:S(2)}) collective-permute-start(f32[2,8,32,128]{3,2,1,0:T(8,128)} %get-tuple-element.146), channel_id=1, source_target_pairs={{0,13},{1,12},{2,15},{3,14},{4,9},{5,8},{6,11},{7,10},{8,5},{9,4},... | collective-permute-start | bytes 786440 | tf_op jit(solution)/shard_map/ppermute | solution.py:226
  81.2 39.3 %collective-permute-start.13 = (f32[2,8,32,128]{3,2,1,0:T(8,128)}, f32[2,8,32,128]{3,2,1,0:T(8,128)}, u32[]{:S(2)}, u32[]{:S(2)}) collective-permute-start(f32[2,8,32,128]{3,2,1,0:T(8,128)} %get-tuple-element.147), channel_id=1, source_target_pairs={{0,14},{1,15},{2,12},{3,13},{4,10},{5,11},{6,8},{7,9},{8,6},{9,7},... | collective-permute-start | bytes 786440 | tf_op jit(solution)/shard_map/ppermute | solution.py:226
  137.4 103.4 %collective-permute-start.15 = (f32[2,64,32,128]{3,2,1,0:T(8,128)}, f32[2,64,32,128]{3,2,1,0:T(8,128)S(1)}, u32[]{:S(2)}, u32[]{:S(2)}) collective-permute-start(f32[2,64,32,128]{3,2,1,0:T(8,128)} %get-tuple-element.152), channel_id=1, source_target_pairs={{0,16},{16,0},{1,17},{17,1},{2,18},{18,2},{3,19},{19,3},{4,20},{20... | collective-permute-start | bytes 6291464 | tf_op jit(solution)/shard_map/ppermute | solution.py:316
  157.6 39.1 %collective-permute-start.24 = (f32[2,8,32,128]{3,2,1,0:T(8,128)}, f32[2,8,32,128]{3,2,1,0:T(8,128)}, u32[]{:S(2)}, u32[]{:S(2)}) collective-permute-start(f32[2,8,32,128]{3,2,1,0:T(8,128)} %get-tuple-element.162), channel_id=1, source_target_pairs={{0,9},{1,8},{2,11},{3,10},{4,13},{5,12},{6,15},{7,14},{8,1},{9,0},... | collective-permute-start | bytes 786440 | tf_op jit(solution)/shard_map/ppermute | solution.py:226
  168.6 39.2 %collective-permute-start.25 = (f32[2,8,32,128]{3,2,1,0:T(8,128)}, f32[2,8,32,128]{3,2,1,0:T(8,128)}, u32[]{:S(2)}, u32[]{:S(2)}) collective-permute-start(f32[2,8,32,128]{3,2,1,0:T(8,128)} %get-tuple-element.163), channel_id=1, source_target_pairs={{0,10},{1,11},{2,8},{3,9},{4,14},{5,15},{6,12},{7,13},{8,2},{9,3},... | collective-permute-start | bytes 786440 | tf_op jit(solution)/shard_map/ppermute | solution.py:226
  174.4 39.2 %collective-permute-start.26 = (f32[2,8,32,128]{3,2,1,0:T(8,128)}, f32[2,8,32,128]{3,2,1,0:T(8,128)}, u32[]{:S(2)}, u32[]{:S(2)}) collective-permute-start(f32[2,8,32,128]{3,2,1,0:T(8,128)} %get-tuple-element.164), channel_id=1, source_target_pairs={{0,11},{1,10},{2,9},{3,8},{4,15},{5,14},{6,13},{7,12},{8,3},{9,2},... | collective-permute-start | bytes 786440 | tf_op jit(solution)/shard_map/ppermute | solution.py:226
  176.5 62.3 %collective-permute-start.27 = (f32[2,8,32,128]{3,2,1,0:T(8,128)}, f32[2,8,32,128]{3,2,1,0:T(8,128)S(1)}, u32[]{:S(2)}, u32[]{:S(2)}) collective-permute-start(f32[2,8,32,128]{3,2,1,0:T(8,128)} %get-tuple-element.165), channel_id=1, source_target_pairs={{0,12},{1,13},{2,14},{3,15},{4,8},{5,9},{6,10},{7,11},{8,4},{9,5},... | collective-permute-start | bytes 786440 | tf_op jit(solution)/shard_map/ppermute | solution.py:226
  196.7 43.9 %collective-permute-start.28 = (f32[2,8,32,128]{3,2,1,0:T(8,128)}, f32[2,8,32,128]{3,2,1,0:T(8,128)}, u32[]{:S(2)}, u32[]{:S(2)}) collective-permute-start(f32[2,8,32,128]{3,2,1,0:T(8,128)} %get-tuple-element.166), channel_id=1, source_target_pairs={{0,13},{1,12},{2,15},{3,14},{4,9},{5,8},{6,11},{7,10},{8,5},{9,4},... | collective-permute-start | bytes 786440 | tf_op jit(solution)/shard_map/ppermute | solution.py:226
  259.0 187.7 %collective-permute-start.31 = (f32[2,64,32,128]{3,2,1,0:T(8,128)}, f32[2,64,32,128]{3,2,1,0:T(8,128)S(1)}, u32[]{:S(2)}, u32[]{:S(2)}) collective-permute-start(f32[2,64,32,128]{3,2,1,0:T(8,128)} %get-tuple-element.171), channel_id=1, source_target_pairs={{0,16},{16,0},{1,17},{17,1},{2,18},{18,2},{3,19},{19,3},{4,20},{20... | collective-permute-start | bytes 6291464 | tf_op jit(solution)/shard_map/ppermute | solution.py:316
  299.5 44.0 %collective-permute-start.55 = (f32[2,8,32,128]{3,2,1,0:T(8,128)}, f32[2,8,32,128]{3,2,1,0:T(8,128)}, u32[]{:S(2)}, u32[]{:S(2)}) collective-permute-start(f32[2,8,32,128]{3,2,1,0:T(8,128)} %get-tuple-element.198), channel_id=1, source_target_pairs={{0,9},{1,8},{2,11},{3,10},{4,13},{5,12},{6,15},{7,14},{8,1},{9,0},... | collective-permute-start | bytes 786440 | tf_op jit(solution)/shard_map/ppermute | solution.py:226
  313.0 36.5 %collective-permute-start.56 = (f32[2,8,32,128]{3,2,1,0:T(8,128)}, f32[2,8,32,128]{3,2,1,0:T(8,128)}, u32[]{:S(2)}, u32[]{:S(2)}) collective-permute-start(f32[2,8,32,128]{3,2,1,0:T(8,128)} %get-tuple-element.199), channel_id=1, source_target_pairs={{0,10},{1,11},{2,8},{3,9},{4,14},{5,15},{6,12},{7,13},{8,2},{9,3},... | collective-permute-start | bytes 786440 | tf_op jit(solution)/shard_map/ppermute | solution.py:226
  318.5 36.4 %collective-permute-start.57 = (f32[2,8,32,128]{3,2,1,0:T(8,128)}, f32[2,8,32,128]{3,2,1,0:T(8,128)}, u32[]{:S(2)}, u32[]{:S(2)}) collective-permute-start(f32[2,8,32,128]{3,2,1,0:T(8,128)} %get-tuple-element.200), channel_id=1, source_target_pairs={{0,11},{1,10},{2,9},{3,8},{4,15},{5,14},{6,13},{7,12},{8,3},{9,2},... | collective-permute-start | bytes 786440 | tf_op jit(solution)/shard_map/ppermute | solution.py:226
  322.2 46.8 %collective-permute-start.58 = (f32[2,8,32,128]{3,2,1,0:T(8,128)}, f32[2,8,32,128]{3,2,1,0:T(8,128)}, u32[]{:S(2)}, u32[]{:S(2)}) collective-permute-start(f32[2,8,32,128]{3,2,1,0:T(8,128)} %get-tuple-element.201), channel_id=1, source_target_pairs={{0,12},{1,13},{2,14},{3,15},{4,8},{5,9},{6,10},{7,11},{8,4},{9,5},... | collective-permute-start | bytes 786440 | tf_op jit(solution)/shard_map/ppermute | solution.py:226
  343.5 81.7 %collective-permute-start.39 = (f32[2,8,32,128]{3,2,1,0:T(8,128)}, f32[2,8,32,128]{3,2,1,0:T(8,128)}, u32[]{:S(2)}, u32[]{:S(2)}) collective-permute-start(f32[2,8,32,128]{3,2,1,0:T(8,128)} %get-tuple-element.180), channel_id=1, source_target_pairs={{0,8},{1,9},{2,10},{3,11},{4,12},{5,13},{6,14},{7,15},{8,0},{9,1},... | collective-permute-start | bytes 786440 | tf_op jit(solution)/shard_map/ppermute | solution.py:226
  349.5 41.5 %collective-permute-start.59 = (f32[2,8,32,128]{3,2,1,0:T(8,128)}, f32[2,8,32,128]{3,2,1,0:T(8,128)S(1)}, u32[]{:S(2)}, u32[]{:S(2)}) collective-permute-start(f32[2,8,32,128]{3,2,1,0:T(8,128)} %get-tuple-element.202), channel_id=1, source_target_pairs={{0,13},{1,12},{2,15},{3,14},{4,9},{5,8},{6,11},{7,10},{8,5},{9,4},... | collective-permute-start | bytes 786440 | tf_op jit(solution)/shard_map/ppermute | solution.py:226
  354.9 47.4 %collective-permute-start.60 = (f32[2,8,32,128]{3,2,1,0:T(8,128)}, f32[2,8,32,128]{3,2,1,0:T(8,128)S(1)}, u32[]{:S(2)}, u32[]{:S(2)}) collective-permute-start(f32[2,8,32,128]{3,2,1,0:T(8,128)} %get-tuple-element.203), channel_id=1, source_target_pairs={{0,14},{1,15},{2,12},{3,13},{4,10},{5,11},{6,8},{7,9},{8,6},{9,7},... | collective-permute-start | bytes 786440 | tf_op jit(solution)/shard_map/ppermute | solution.py:226
  369.0 44.6 %collective-permute-start.61 = (f32[2,8,32,128]{3,2,1,0:T(8,128)}, f32[2,8,32,128]{3,2,1,0:T(8,128)S(1)}, u32[]{:S(2)}, u32[]{:S(2)}) collective-permute-start(f32[2,8,32,128]{3,2,1,0:T(8,128)} %get-tuple-element.204), channel_id=1, source_target_pairs={{0,15},{1,14},{2,13},{3,12},{4,11},{5,10},{6,9},{7,8},{8,7},{9,6},... | collective-permute-start | bytes 786440 | tf_op jit(solution)/shard_map/ppermute | solution.py:226
  425.2 106.8 %collective-permute-start.76 = (f32[2,64,32,128]{3,2,1,0:T(8,128)}, f32[2,64,32,128]{3,2,1,0:T(8,128)}, u32[]{:S(2)}, u32[]{:S(2)}) collective-permute-start(f32[2,64,32,128]{3,2,1,0:T(8,128)} %get-tuple-element.229), channel_id=1, source_target_pairs={{0,16},{16,0},{1,17},{17,1},{2,18},{18,2},{3,19},{19,3},{4,20},{20... | collective-permute-start | bytes 6291464 | tf_op jit(solution)/shard_map/ppermute | solution.py:316
  429.9 40.1 %collective-permute-start.44 = (f32[2,8,32,128]{3,2,1,0:T(8,128)}, f32[2,8,32,128]{3,2,1,0:T(8,128)}, u32[]{:S(2)}, u32[]{:S(2)}) collective-permute-start(f32[2,8,32,128]{3,2,1,0:T(8,128)} %get-tuple-element.185), channel_id=1, source_target_pairs={{0,13},{1,12},{2,15},{3,14},{4,9},{5,8},{6,11},{7,10},{8,5},{9,4},... | collective-permute-start | bytes 786440 | tf_op jit(solution)/shard_map/ppermute | solution.py:226
  491.6 71.8 %collective-permute-start.75 = (f32[2,64,32,128]{3,2,1,0:T(8,128)}, f32[2,64,32,128]{3,2,1,0:T(8,128)}, u32[]{:S(2)}, u32[]{:S(2)}) collective-permute-start(f32[2,64,32,128]{3,2,1,0:T(8,128)} %get-tuple-element.227), channel_id=1, source_target_pairs={{0,16},{16,0},{1,17},{17,1},{2,18},{18,2},{3,19},{19,3},{4,20},{20... | collective-permute-start | bytes 6291464 | tf_op jit(solution)/shard_map/ppermute | solution.py:316
  (101 other events, 3073.0 us)
